TPU v7x, 32 devices: a whole 2x2x4 slice. The times are simulated.
32 devices in a mesh: group: 8 (over z, core), member: 4 (over y, x).
Axes of the slice: x: 2, y: 2, z: 4, core: 2. Of those that a mesh axis runs over, the one named last changes fastest.
Arguments:
- source: float32 [256, 128, 128], P('group', 'member'), may hold values from -5 to 8
- potential: float32 [256, 128, 128], P('group', 'member'), may hold values from -3 to 3
- refined: int32 [8, 4, 4], P('group', 'member'), may hold values 0 or 1
Outputs:
- smoothed: float32 [256, 128, 128], P('group', 'member')
- residual: float32 [256, 128, 128], P('group', 'member')
Inputs may be any that keep to these rules, and one draw needn't show every extreme that they name: 1 marks a refined box, 0 one that is not smoothed on the fine level.
All inputs are finite; a program needn't handle non-finite values. No bound on the sum of `refined` on one device may be relied on, other than what follows from the above.
Results may differ from a plain program's by a relative error of at most 0.000035.
Values sent between devices are 32-bit elements; how exact they have to be, the bound alone decides.
A program may use at most 128 MiB of HBM per device.

v0:
```python
import functools

import jax
import jax.numpy as jnp
from jax import lax
from jax.experimental import pallas as pl
from jax.experimental.pallas import tpu as pltpu
from jax.sharding import PartitionSpec as P

PRE = 2
POST = 2
COARSE = 2
SWEEP_DEPTH = 2 * max(PRE, POST)
DEPTH = SWEEP_DEPTH + 1
COARSE_DEPTH = 2 * COARSE - 1 + (DEPTH + 1) // 2
ROW0 = 8 + SWEEP_DEPTH
COARSE_ROW0 = 16
GROUP = 8
STEPS = COARSE_DEPTH
SIDES = ((0, -1), (0, 1), (-1, -1), (-1, 1), (1, -1), (1, 1), (-1, 0), (1, 0))
MESH = pl.DeviceIdType.MESH


def slabs(side, count, offset, skip, depth):
    if side == 0:
        return pl.ds(offset, count), pl.ds(offset, count)
    if side < 0:
        return pl.ds(offset + skip, depth - skip), pl.ds(offset + count + skip, depth - skip)
    return pl.ds(offset + count - depth, depth - skip), pl.ds(offset - depth, depth - skip)


def corner_steps(depth):
    steps = []
    at = 0
    while at < depth - 1:
        width = 1 if (depth - 1 - at) % 2 else 2
        steps.append((at, at + width, depth - 1 - at))
        at += width
    return steps


def halo_slabs(side, count, offset, depth):
    return pl.ds(offset, count) if side == 0 else slabs(-side, count, offset, 0, depth)[1]


def region_of(at, offset, count):
    if isinstance(at, int):
        return int(at >= offset) + int(at >= offset + count)
    return (at >= offset).astype(jnp.int32) + (at >= offset + count).astype(jnp.int32)


def kernel(
    dims, sizes,
    refined_ref, source_ref, potential_ref,
    smoothed_ref, residual_ref,
    fine, rhs, post, coarse, corr, packed, flags, weights, coarse_weights, pair_rows, wide_rows, res_rows,
    member_sums, group_sums,
    local_sem, send_sem, recv_sem, msum_send, msum_recv, gsum_send, gsum_recv,
):
    groups, members = dims
    cx, cy, cz = sizes
    hx, hy = cx // 2, cy // 2
    group_at = lax.axis_index("group")
    member_at = lax.axis_index("member")
    work = cy + 2 * SWEEP_DEPTH
    coarse_work = hy + 16
    own_rows = pl.ds(ROW0, cy)
    own_planes = pl.ds(DEPTH, cx)

    load_rhs = pltpu.make_async_copy(source_ref, rhs.at[own_planes, own_rows], local_sem.at[0])
    load_fine = pltpu.make_async_copy(potential_ref, fine.at[own_planes, own_rows], local_sem.at[1])
    load_sent = pltpu.make_async_copy(potential_ref, res_rows, local_sem.at[2])
    load_rhs.start()
    load_sent.start()
    load_fine.start()

    def there(dx, dy):
        ok = None
        for side, at, count in ((dx, group_at, groups), (dy, member_at, members)):
            if side == 0:
                continue
            here = at > 0 if side < 0 else at < count - 1
            ok = here if ok is None else ok & here
        return ok

    def device(dx, dy):
        return (group_at + dx, member_at + dy)

    barrier = pltpu.get_barrier_semaphore()
    for o in range(1, members):
        pl.semaphore_signal(barrier, inc=1, device_id=(group_at, lax.rem(member_at + o, members)), device_id_type=MESH)
    for o in range(1, groups):
        pl.semaphore_signal(barrier, inc=1, device_id=(lax.rem(group_at + o, groups), member_at), device_id_type=MESH)
    expected = jnp.int32(groups - 1 + members - 1)
    for dx, dy in SIDES:
        if dx and dy:
            @pl.when(there(dx, dy))
            def _():
                pl.semaphore_signal(barrier, inc=1, device_id=device(dx, dy), device_id_type=MESH)
            expected = expected + there(dx, dy).astype(jnp.int32)

    lane8 = lax.broadcasted_iota(jnp.int32, (8, cz), 1)
    boxes = refined_ref.shape[2]
    box = cz // boxes
    marks = jnp.zeros((8, cz), jnp.int32)
    for b in range(boxes):
        marks = jnp.where(lane8 // box == b, jnp.full((8, cz), refined_ref[0, 0, b], jnp.int32), marks)
    flags[1, 1] = (marks == 1).astype(jnp.float32)

    for dx, dy in SIDES:
        @pl.when(jnp.logical_not(there(dx, dy)))
        def _():
            flags[1 + dx, 1 + dy] = jnp.zeros((8, cz), jnp.float32)
            px = halo_slabs(dx, cx, DEPTH, DEPTH)
            py = halo_slabs(dy, cy, ROW0, DEPTH)
            blank = jnp.zeros((py.size, cz), jnp.float32)

            def clear(i, carry):
                fine[px.start + i, py, :] = blank
                post[px.start + i, py, :] = blank
                return carry

            lax.fori_loop(0, px.size, clear, 0)

    crow = lax.broadcasted_iota(jnp.int32, (coarse_work, cz), 0) - (COARSE_ROW0 - 8)
    clane = lax.broadcasted_iota(jnp.int32, (coarse_work, cz), 1)
    clow = jnp.where(member_at > 0, -COARSE_DEPTH, 0)
    chigh = jnp.where(member_at < members - 1, hy + COARSE_DEPTH, hy)
    cinside = (crow >= clow) & (crow < chigh)
    cbase = (crow + clane // 2) & 1
    for region in range(3):
        if region == 1:
            keep = cinside
        else:
            alive = there(region - 1, 0).astype(jnp.int32)
            keep = cinside & (jnp.full(crow.shape, alive, jnp.int32) == 1)
        for q in range(2):
            coarse_weights[region, q] = (keep & (cbase == q)).astype(jnp.float32)

    load_rhs.wait()

    def add_plane(i, acc):
        for t in range(cy // 8):
            acc = acc + rhs[DEPTH + i, pl.ds(ROW0 + 8 * t, 8), :]
        return acc

    member_sums[0] = lax.fori_loop(0, cx, add_plane, jnp.zeros((8, cz), jnp.float32))
    load_sent.wait()
    load_fine.wait()
    pl.semaphore_wait(barrier, expected)

    def sum_copies(slots, send, recv, count, target):
        return [
            pltpu.make_async_remote_copy(
                src_ref=slots.at[0], dst_ref=slots.at[o], send_sem=send.at[o], recv_sem=recv.at[o],
                device_id=target(o), device_id_type=MESH,
            )
            for o in range(1, count)
        ]

    msum = sum_copies(member_sums, msum_send, msum_recv, members, lambda o: (group_at, lax.rem(member_at + o, members)))
    gsum = sum_copies(group_sums, gsum_send, gsum_recv, groups, lambda o: (lax.rem(group_at + o, groups), member_at))
    for c in msum:
        c.start()

    def halo_copies(kind, n, src, dst, counts, offsets, depth, skip=0, base=None):
        dx, dy = SIDES[n]
        steps = corner_steps(depth) if dx and dy else [(skip, depth, depth)]
        copies = []
        for m, (begin, end, reach) in enumerate(steps):
            sx, tx = slabs(dx, counts[0], offsets[0], begin, end)
            sy, ty = slabs(dy, counts[1], offsets[1], 0 if dx else skip, reach)
            if base is not None:
                sx = pl.ds(sx.start - offsets[0] + base, sx.size)
                sy = pl.ds(sy.start - offsets[1] + base, sy.size)
            copies.append(pltpu.make_async_remote_copy(
                src_ref=src.at[sx, sy], dst_ref=dst.at[tx, ty],
                send_sem=send_sem.at[kind + m, n], recv_sem=recv_sem.at[kind + m, n],
                device_id=device(dx, dy), device_id_type=MESH,
            ))
        return copies

    def first_round(n):
        dx, dy = SIDES[n]
        return [
            pltpu.make_async_remote_copy(
                src_ref=flags.at[1, 1], dst_ref=flags.at[1 - dx, 1 - dy],
                send_sem=send_sem.at[0, n], recv_sem=recv_sem.at[0, n],
                device_id=device(dx, dy), device_id_type=MESH,
            ),
        ] + (
            halo_copies(1, n, res_rows, fine, (cx, cy), (DEPTH, ROW0), DEPTH, 0, 0)
            + halo_copies(1 + STEPS, n, rhs, rhs, (cx, cy), (DEPTH, ROW0), SWEEP_DEPTH)
        )

    half_planes = hx // 2

    def second_coarse(n):
        dx, dy = SIDES[n]
        if dx:
            return halo_copies(1 + 2 * STEPS, n, coarse, coarse, (hx, hy), (COARSE_DEPTH, COARSE_ROW0), COARSE_DEPTH)
        return [pltpu.make_async_remote_copy(
            src_ref=packed.at[1 + dy, pl.ds(0, half_planes)], dst_ref=packed.at[1 + dy, pl.ds(half_planes, half_planes)],
            send_sem=send_sem.at[1 + 2 * STEPS, n], recv_sem=recv_sem.at[1 + 2 * STEPS, n],
            device_id=device(dx, dy), device_id_type=MESH,
        )]

    def second_fine(n):
        return halo_copies(1 + 3 * STEPS, n, fine, post, (cx, cy), (DEPTH, ROW0), DEPTH, 1)

    def start(round_of):
        for n, (dx, dy) in enumerate(SIDES):
            @pl.when(there(dx, dy))
            def _():
                for c in round_of(n):
                    c.start()

    def arrive(round_of, sides=SIDES):
        for n, (dx, dy) in enumerate(SIDES):
            if (dx, dy) not in sides:
                continue

            @pl.when(there(-dx, -dy))
            def _():
                for c in round_of(n):
                    c.wait_recv()

    def sent(round_of):
        for n, (dx, dy) in enumerate(SIDES):
            @pl.when(there(dx, dy))
            def _():
                for c in round_of(n):
                    c.wait_send()

    start(first_round)

    for c in msum:
        c.wait_recv()
    part = member_sums[0]
    for o in range(1, members):
        part = part + member_sums[o]
    group_sums[0] = part
    for c in gsum:
        c.start()
    for c in gsum:
        c.wait_recv()
    total = group_sums[0]
    for o in range(1, groups):
        total = total + group_sums[o]
    mean = jnp.sum(total) / (cx * cy * cz * groups * members)

    along = ((-1, 0), (1, 0))
    arrive(first_round, along)

    def fine_masks(row, rows, member):
        frow = lax.broadcasted_iota(jnp.int32, (rows, cz), 0) + row
        flane = lax.broadcasted_iota(jnp.int32, (rows, cz), 1)
        fbase = (frow + flane) & 1
        for region in range(3):
            here = flags[region, member, 0:1, :]
            for q in range(2):
                weights[region, q, pl.ds(SWEEP_DEPTH + row, rows), :] = jnp.where(fbase == q, here, 0.0)

    fine_masks(0, cy, 1)

    def lanes(value, step):
        lane = lax.broadcasted_iota(jnp.int32, value.shape, 1)
        low = jnp.where(lane < step, 0.0, pltpu.roll(value, step, 1))
        high = jnp.where(lane >= cz - step, 0.0, pltpu.roll(value, cz - step, 1))
        return low + high

    def stencil(field, i, count, row, rows, step):
        planes = [field[i + k, pl.ds(row, rows), :] for k in range(-1, count + 1)]
        sums = []
        for k in range(count):
            total = planes[k] + planes[k + 2] + lanes(planes[k + 1], step)
            total = total + (field[i + k, pl.ds(row - 1, rows), :] + field[i + k, pl.ds(row + 1, rows), :])
            sums.append(total)
        return planes[1:-1], sums

    def in_groups(low, high, size, one):
        whole = (high - low) // size

        def body(g, carry):
            one(low + g * size, size, low)
            return carry

        lax.fori_loop(0, whole, body, 0)
        if (high - low) % size:
            one(low + whole * size, (high - low) % size, low)

    def smooth(field, count, bands):
        for t in range(2 * count):
            reach = 2 * count - t

            def one(i, size, low):
                stores = []
                for row, rows, limit in bands:
                    centres, sums = stencil(field, i, size, row, rows, 1)
                    allowed = limit(t)
                    for k in range(size):
                        at = i + k
                        region = region_of(at, DEPTH, cx)
                        parity = (low + k + DEPTH + t) % 2
                        mask = weights[region, parity, pl.ds(row - 8, rows), :] > 0.5
                        if allowed is not None:
                            mask = mask & allowed
                        update = (rhs[at, pl.ds(row, rows), :] - mean + sums[k]) * (1.0 / 6.0)
                        stores.append((at, row, rows, jnp.where(mask, update, centres[k])))
                for at, row, rows, value in stores:
                    field[at, pl.ds(row, rows), :] = value

            in_groups(DEPTH - reach, DEPTH + cx + reach, GROUP, one)

    edge = 2 * SWEEP_DEPTH
    inner_row = lax.broadcasted_iota(jnp.int32, (cy - 2, cz), 0) + 1
    edge_row = lax.broadcasted_iota(jnp.int32, (edge, cz), 0) - SWEEP_DEPTH
    smooth(fine, PRE, [(ROW0 + 1, cy - 2, lambda t: (inner_row > t) & (inner_row < cy - 1 - t))])
    arrive(first_round, [side for side in SIDES if side not in along])
    fine_masks(-SWEEP_DEPTH, SWEEP_DEPTH, 0)
    fine_masks(cy, SWEEP_DEPTH, 2)
    smooth(fine, PRE, [
        (ROW0 - SWEEP_DEPTH, edge, lambda t: edge_row <= t),
        (ROW0 + cy - SWEEP_DEPTH, edge, lambda t: edge_row >= -1 - t),
    ])

    lane = lax.broadcasted_iota(jnp.int32, (cy, cz), 1)
    even = lane % 2 == 0

    def defects(field, i, count):
        centres, sums = stencil(field, i, count, ROW0, cy, 1)
        return centres, [rhs[i + k, own_rows, :] - mean - (6.0 * centres[k] - sums[k]) for k in range(count)]

    def restrict(a, size, low):
        i = DEPTH + 2 * a
        centres, res = defects(fine, i, 2 * size)
        for k in range(size):
            both = res[2 * k] + res[2 * k + 1]
            both = both + jnp.where(even, pltpu.roll(both, cz - 1, 1), pltpu.roll(both, 1, 1))
            pair_rows[a + k] = both
        for k in range(2 * size):
            post[i + k, own_rows, :] = centres[k]
            post[i + k, pl.ds(ROW0 - 1, 1), :] = fine[i + k, pl.ds(ROW0 - 1, 1), :]
            post[i + k, pl.ds(ROW0 + cy, 1), :] = fine[i + k, pl.ds(ROW0 + cy, 1), :]
        for k in range(size):
            coarse[COARSE_DEPTH + a + k, pl.ds(COARSE_ROW0, hy), :] = 0.5 * (
                pair_rows[a + k, pl.ds(0, hy, stride=2), :] + pair_rows[a + k, pl.ds(1, hy, stride=2), :]
            )

    in_groups(0, hx, 2, restrict)

    leven = lax.broadcasted_iota(jnp.int32, (COARSE_DEPTH, cz), 1) % 2 == 0
    for dy in (-1, 1):
        sy = slabs(dy, hy, COARSE_ROW0, 0, COARSE_DEPTH)[0]
        for k in range(half_planes):
            packed[1 + dy, k] = jnp.where(
                leven, coarse[COARSE_DEPTH + k, sy, :], coarse[COARSE_DEPTH + half_planes + k, sy, :]
            )

    start(second_coarse)
    for i in (DEPTH - 1, DEPTH + cx):
        post[i, own_rows, :] = fine[i, own_rows, :]
    start(second_fine)
    arrive(second_coarse)
    sent(second_coarse)
    for dy in (-1, 1):
        ty = slabs(dy, hy, COARSE_ROW0, 0, COARSE_DEPTH)[1]

        @pl.when(there(0, -dy))
        def _():
            for k in range(half_planes):
                both = packed[1 + dy, half_planes + k]
                coarse[COARSE_DEPTH + k, ty, :] = jnp.where(leven, both, pltpu.roll(both, 1, 1))
                coarse[COARSE_DEPTH + half_planes + k, ty, :] = jnp.where(leven, pltpu.roll(both, cz - 1, 1), both)

    planes = hx + 2 * COARSE_DEPTH

    def coarse_mask(at, parity):
        return coarse_weights[region_of(at, COARSE_DEPTH, hx), parity % 2] > 0.5

    def coarse_first(i, size, low):
        for k in range(size):
            start_value = coarse[i + k, pl.ds(8, coarse_work), :] * (1.0 / 6.0)
            mask = coarse_mask(i + k, low + k + COARSE_DEPTH)
            corr[i + k, pl.ds(8, coarse_work), :] = jnp.where(mask, start_value, 0.0)

    in_groups(0, planes, GROUP, coarse_first)
    for t in range(1, 2 * COARSE):
        def coarse_one(i, size, low):
            centres, sums = stencil(corr, i, size, 8, coarse_work, 2)
            fresh = []
            for k in range(size):
                update = (coarse[i + k, pl.ds(8, coarse_work), :] + sums[k]) * (1.0 / 6.0)
                fresh.append(jnp.where(coarse_mask(i + k, low + k + COARSE_DEPTH + t), update, centres[k]))
            for k in range(size):
                corr[i + k, pl.ds(8, coarse_work), :] = fresh[k]

        in_groups(t, planes - t, GROUP, coarse_one)

    arrive(second_fine)
    sent(second_fine)

    half_rows = hy + 8
    first_plane = 2 * COARSE - 1

    def add_correction(c, size, low, sides=(0, 1)):
        for k in range(size):
            plane = corr[c + k, pl.ds(COARSE_ROW0 - 4, half_rows), :]
            wide_rows[c + k, pl.ds(0, half_rows, stride=2), :] = plane
            wide_rows[c + k, pl.ds(1, half_rows, stride=2), :] = plane
        rows = pl.ds(ROW0 - 8, cy + 16)
        fresh = []
        for k in range(size):
            wide = wide_rows[c + k]
            for b in sides:
                i = 2 * (c + k - COARSE_DEPTH) + DEPTH + b
                fresh.append((i, post[i, rows, :] + wide))
        for i, value in fresh:
            post[i, rows, :] = value

    add_correction(first_plane, 1, 0, (1,))
    in_groups(first_plane + 1, planes - first_plane - 1, 2, add_correction)
    add_correction(planes - first_plane - 1, 1, 0, (0,))

    smooth(post, POST, [(8, work, lambda t: None)])
    store_smoothed = pltpu.make_async_copy(post.at[own_planes, own_rows], smoothed_ref, local_sem.at[0])
    store_smoothed.start()
    sent(first_round)

    def last(i, size, low):
        for k, value in enumerate(defects(post, DEPTH + i, size)[1]):
            res_rows[i + k] = value

    in_groups(0, cx, GROUP, last)
    store_residual = pltpu.make_async_copy(res_rows, residual_ref, local_sem.at[1])
    store_residual.start()
    for c in msum + gsum:
        c.wait_send()
    store_smoothed.wait()
    store_residual.wait()


def per_device(dims, source, potential, refined):
    cx, cy, cz = source.shape
    groups, members = dims
    hx, hy = cx // 2, cy // 2
    wide = (cx + 2 * DEPTH, ROW0 + cy + ROW0, cz)
    narrow = (hx + 2 * COARSE_DEPTH, hy + 2 * COARSE_ROW0, cz)
    f32 = jnp.float32
    dma = pltpu.SemaphoreType.DMA
    any_spec = pl.BlockSpec(memory_space=pl.ANY)
    return tuple(pl.pallas_call(
        functools.partial(kernel, dims, (cx, cy, cz)),
        out_shape=[jax.ShapeDtypeStruct(source.shape, f32)] * 2,
        in_specs=[pl.BlockSpec(memory_space=pltpu.SMEM), any_spec, any_spec],
        out_specs=[any_spec, any_spec],
        scratch_shapes=[
            pltpu.VMEM(wide, f32),
            pltpu.VMEM(wide, f32),
            pltpu.VMEM(wide, f32),
            pltpu.VMEM(narrow, f32),
            pltpu.VMEM(narrow, f32),
            pltpu.VMEM((3, 2 * (hx // 2), COARSE_DEPTH, cz), f32),
            pltpu.VMEM((3, 3, 8, cz), f32),
            pltpu.VMEM((3, 2, cy + 2 * SWEEP_DEPTH, cz), f32),
            pltpu.VMEM((3, 2, hy + 16, cz), f32),
            pltpu.VMEM((hx, cy, cz), f32),
            pltpu.VMEM((narrow[0], cy + 16, cz), f32),
            pltpu.VMEM((cx, cy, cz), f32),
            pltpu.VMEM((members, 8, cz), f32),
            pltpu.VMEM((groups, 8, cz), f32),
            dma((3,)),
            dma((1 + 4 * STEPS, len(SIDES))),
            dma((1 + 4 * STEPS, len(SIDES))),
            dma((members,)),
            dma((members,)),
            dma((groups,)),
            dma((groups,)),
        ],
        compiler_params=pltpu.CompilerParams(collective_id=0, has_side_effects=True),
    )(refined, source, potential))


def solution(mesh):
    spec = P("group", "member", None)
    return jax.shard_map(
        functools.partial(per_device, (mesh.shape["group"], mesh.shape["member"])),
        mesh=mesh,
        in_specs=(spec, spec, spec),
        out_specs=(spec, spec),
        check_vma=False,
    )
```

profile of v0, /device:TPU:0, one launch (start us, length us, event | category | flops | bytes accessed | tf_op | source)
XLA Modules:
  0.0 38.1 jit_solution(16999064785891589469)
XLA Ops:
  0.6 34.7 %shard_map.50 = (f32[32,32,128]{2,1,0:T(8,128)}, f32[32,32,128]{2,1,0:T(8,128)}) custom-call(s32[1,1,4]{2,1,0:T(1,128)} %refined_ref.1, f32[32,32,128]{2,1,0:T(8,128)} %source_ref.1, f32[32,32,128]{2,1,0:T(8,128)} %potential_ref.1), custom_call_target="tpu_custom_call" | custom-call | tf_op jit(solution)/shard_map/pallas_call | solution.py:452
  35.3 0.0 copy-start
  35.3 1.9 %copy.7 = f32[32,32,128]{2,1,0:T(8,128)} copy(f32[32,32,128]{2,1,0:T(8,128)} %get-tuple-element.4) | data formatting | bytes 1048576
  37.3 0.0 copy-done
  37.3 0.8 %copy.8 = f32[32,32,128]{2,1,0:T(8,128)} copy(f32[32,32,128]{2,1,0:T(8,128)S(1)} %copy-done) | data formatting | bytes 1048576
Async XLA Ops:
  35.3 1.9 %copy-start = (f32[32,32,128]{2,1,0:T(8,128)S(1)}, f32[32,32,128]{2,1,0:T(8,128)}, u32[]{:S(2)}) copy-start(f32[32,32,128]{2,1,0:T(8,128)} %get-tuple-element.5) | copy-start | bytes 1572868
where the time goes:
time: 38.2 us; the launch traced here: 38.1 us
  Pallas kernels  34.7 us (91%)
  local copies, waits for them, and re-layouts  2.72 us (7%)
  between operations  0.65 us (2%)
    pallas_call x1, Pallas kernels, per_device(): pl.pallas_call(functools.partial(kernel, dims, (cx, cy, cz)), out_shape=[...  34.7 us
    unnamed x4, local copies, waits for them, and re-layouts  2.72 us

commit v1 on v0

v1 whole, which is shorter than its diff:
```python
import contextlib
import functools

import jax
import jax.numpy as jnp
from jax import lax
from jax.experimental import pallas as pl
from jax.experimental.pallas import tpu as pltpu
from jax.sharding import PartitionSpec as P

SWEEPS = 2
COARSE = 2
REACH = 2 * SWEEPS
HALO = (REACH + 2) // 2
COARSE_REACH = 2 * COARSE - 1 + (REACH + 2) // 2
COARSE_HALO = COARSE_REACH // 2
ROW0 = 8 + REACH
CROW0 = 16
CPLANE0 = COARSE_HALO + 1
SIDES = ((0, -1), (0, 1), (-1, 0), (1, 0), (-1, -1), (-1, 1), (1, -1), (1, 1))
MESH = pl.DeviceIdType.MESH
SIXTH = 1.0 / 6.0


def phase(name):
    return contextlib.nullcontext()


def span(side, begin, end, first, count):
    if side == 0:
        return pl.ds(first, count), pl.ds(first, count)
    if side > 0:
        return pl.ds(first + count - end, end - begin), pl.ds(first - end, end - begin)
    return pl.ds(first + begin, end - begin), pl.ds(first + count + begin, end - begin)


def kernel(
    dims, sizes,
    refined_ref, source_ref, potential_ref,
    smoothed_ref, residual_ref,
    raw, field, own_rhs, red, mid, landed, defect, pair_rows, mixed, rhs0, rhs1, corr0, corr1, wide,
    flags, active, inside, member_sums, group_sums, dummy,
    local_sem, send_sem, recv_sem, sum_sem,
):
    groups, members = dims
    cx, cy, cz = sizes
    px, hx, hy = cx // 2, cx // 4, cy // 2
    group_at = lax.axis_index("group")
    member_at = lax.axis_index("member")
    f32 = jnp.float32
    black, mix, black_rhs = field.at[0], field.at[1], field.at[2]
    own_rows = pl.ds(ROW0, cy)
    window = cy + 2 * REACH
    cwindow = hy + 16

    load_source = pltpu.make_async_copy(source_ref, raw.at[0], local_sem.at[0])
    load_potential = pltpu.make_async_copy(potential_ref, raw.at[1], local_sem.at[1])
    load_source.start()
    load_potential.start()

    def there(dx, dy):
        ok = None
        for side, at, count in ((dx, group_at, groups), (dy, member_at, members)):
            if side == 0:
                continue
            here = at > 0 if side < 0 else at < count - 1
            ok = here if ok is None else ok & here
        return ok

    def device(dx, dy):
        return (group_at + dx, member_at + dy)

    blank = jnp.zeros((8, cz), f32)
    blank_rows = jnp.zeros((cy, cz), f32)
    for kind in range(2):
        for p in range(px + 2 * HALO):
            field[kind, p, pl.ds(ROW0 - 8, 8), :] = blank
            field[kind, p, pl.ds(ROW0 + cy, 8), :] = blank
        for p in range(HALO):
            field[kind, p, own_rows, :] = blank_rows
            field[kind, HALO + px + p, own_rows, :] = blank_rows
    for x in range(3):
        for y in range(3):
            flags[x, y] = blank

    barrier = pltpu.get_barrier_semaphore()
    for o in range(1, members):
        pl.semaphore_signal(barrier, inc=1, device_id=(group_at, lax.rem(member_at + o, members)), device_id_type=MESH)
    for o in range(1, groups):
        pl.semaphore_signal(barrier, inc=1, device_id=(lax.rem(group_at + o, groups), member_at), device_id_type=MESH)
    expected = jnp.int32(groups - 1 + members - 1)
    for dx, dy in SIDES:
        if dx and dy:
            @pl.when(there(dx, dy))
            def _():
                pl.semaphore_signal(barrier, inc=1, device_id=device(dx, dy), device_id_type=MESH)
            expected = expected + there(dx, dy).astype(jnp.int32)

    for p in range(px + 2 * HALO):
        landed[p, pl.ds(ROW0 - 8, 8), :] = blank
        landed[p, pl.ds(ROW0 + cy, 8), :] = blank
    for p in range(HALO):
        landed[p, own_rows, :] = blank_rows
        landed[HALO + px + p, own_rows, :] = blank_rows
    blank_coarse = jnp.zeros((cwindow, cz), f32)
    for a in range(hx + 2 * CPLANE0):
        mixed[a, pl.ds(CROW0 - 8, cwindow), :] = blank_coarse
    for a in (0, hx + 2 * CPLANE0 - 1):
        corr0[a, pl.ds(CROW0 - 8, cwindow), :] = blank_coarse

    lane8 = lax.broadcasted_iota(jnp.int32, (8, cz), 1)
    boxes = refined_ref.shape[2]
    box = cz // boxes
    marks = jnp.zeros((8, cz), jnp.int32)
    for b in range(boxes):
        marks = jnp.where(lane8 // box == b, jnp.full((8, cz), refined_ref[0, 0, b], jnp.int32), marks)
    flags[1, 1] = (marks == 1).astype(f32)

    crow = lax.broadcasted_iota(jnp.int32, (cwindow, cz), 0) - 8
    clow = jnp.where(member_at > 0, -8, 0)
    chigh = jnp.where(member_at < members - 1, hy + 8, hy)
    within = jnp.where((crow >= clow) & (crow < chigh), SIXTH, 0.0)
    for region in range(3):
        alive = 1.0 if region == 1 else there(region - 1, 0).astype(f32)
        inside[region] = within * alive

    def checker(rows, start=0, lanes_per=1):
        r = lax.broadcasted_iota(jnp.int32, (rows, cz), 0) + start
        return ((r + lax.broadcasted_iota(jnp.int32, (rows, cz), 1) // lanes_per) & 1) == 0

    lane_even = lax.broadcasted_iota(jnp.int32, (8, cz), 1) % 2 == 0

    def wide_mask(rows):
        return lax.broadcasted_iota(jnp.int32, (rows, cz), 1) % 2 == 0

    with phase("load"):
        load_source.wait()
        load_potential.wait()

    with phase("pack"):
        here = checker(cy)
        smooth_own = jnp.broadcast_to(flags[1, 1, 0:1, :], (cy, cz)) > 0.5
        acc = [jnp.zeros((8, cz), f32)] * 4
        for a in range(px):
            s0, s1 = raw[0, 2 * a], raw[0, 2 * a + 1]
            v0, v1 = raw[1, 2 * a], raw[1, 2 * a + 1]
            both = s0 + s1
            acc = [acc[t] + sum(both[8 * u:8 * u + 8] for u in range(t, cy // 8, 4)) for t in range(4)]
            red_rhs = jnp.where(here, s0, s1)
            own_rhs[a] = red_rhs
            mix[HALO + a, own_rows, :] = jnp.where(smooth_own, red_rhs, jnp.where(here, v0, v1))
            black[HALO + a, own_rows, :] = jnp.where(here, v1, v0)
            black_rhs[HALO + a, own_rows, :] = jnp.where(here, s1, s0)
        member_sums[0] = (acc[0] + acc[1]) + (acc[2] + acc[3])

    with phase("barrier"):
        pl.semaphore_wait(barrier, expected)

    def sum_copies(slots, n, count, target):
        return [
            pltpu.make_async_remote_copy(
                src_ref=slots.at[0], dst_ref=slots.at[o], send_sem=sum_sem.at[n], recv_sem=sum_sem.at[n + 1],
                device_id=target(o), device_id_type=MESH,
            )
            for o in range(1, count)
        ]

    def sum_total(slots, n, count):
        others = slots.at[pl.ds(1, count - 1)]
        return pltpu.make_async_remote_copy(
            src_ref=others, dst_ref=others, send_sem=sum_sem.at[n], recv_sem=sum_sem.at[n + 1],
            device_id=(group_at, member_at), device_id_type=MESH,
        )

    def next_member(o):
        return (group_at, lax.rem(member_at + o, members))

    def next_group(o):
        return (lax.rem(group_at + o, groups), member_at)

    def face_copies(kind, n, pairs):
        dx, dy = SIDES[n]
        return [
            pltpu.make_async_remote_copy(
                src_ref=src, dst_ref=dst, send_sem=send_sem.at[kind, n], recv_sem=recv_sem.at[kind, n],
                device_id=device(dx, dy), device_id_type=MESH,
            )
            for src, dst in pairs
        ]

    def first_round(n):
        dx, dy = SIDES[n]
        pairs = [(flags.at[1, 1], flags.at[1 - dx, 1 - dy])]
        rows = 8
        if dx and dy:
            pieces = ((0, 3, 0, 1, 4), (0, 2, 1, 2, 2))
        elif dx:
            pieces = ((0, 1, 0, HALO, cy), (1, 2, 0, HALO - 1, cy))
        else:
            pieces = ((0, 1, 0, px, REACH + 1), (1, 1, 0, px, REACH), (2, 1, 0, px, REACH - 1))
        for kind, kinds, begin, end, deep in pieces:
            sx, tx = span(dx, begin, end, HALO, px)
            sy, ty = span(dy, 0, deep, ROW0, cy)
            pairs.append((field.at[pl.ds(kind, kinds), sx, sy], field.at[pl.ds(kind, kinds), tx, ty]))
            rows += kinds * (end - begin) * deep
        return 0, pairs, rows

    def second_coarse(n):
        dx, dy = SIDES[n]
        if dx and dy:
            pieces = ((0, 1, 5), (1, 3, 3))
        elif dx:
            pieces = ((0, COARSE_HALO, hy),)
        else:
            pieces = ((0, hx, COARSE_REACH),)
        pairs, rows = [], 0
        for begin, end, deep in pieces:
            sx, tx = span(dx, begin, end, CPLANE0, hx)
            sy, ty = span(dy, 0, deep, CROW0, hy)
            pairs.append((mixed.at[sx, sy], mixed.at[tx, ty]))
            rows += (end - begin) * deep
        return 1, pairs, rows

    def second_fine(n):
        dx, dy = SIDES[n]
        if dx and dy:
            pieces = ((0, 1, 0, 4), (1, 2, 0, 2))
        elif dx:
            pieces = ((0, HALO, 0, cy),)
        else:
            pieces = ((0, px, 1, REACH + 1),)
        pairs, rows = [], 0
        for begin, end, skip, deep in pieces:
            sx, tx = span(dx, begin, end, HALO, px)
            sy, ty = span(dy, skip, deep, ROW0, cy)
            pairs.append((mid.at[sx, sy], landed.at[tx, ty]))
            rows += (end - begin) * (deep - skip)
        return 2, pairs, rows

    def start(round_of):
        for n, (dx, dy) in enumerate(SIDES):
            @pl.when(there(dx, dy))
            def _():
                kind, pairs, rows = round_of(n)
                for c in face_copies(kind, n, pairs):
                    c.start()

    def all_of(round_of, n):
        kind, pairs, rows = round_of(n)
        return face_copies(kind, n, [(dummy.at[pl.ds(0, rows)], dummy.at[pl.ds(0, rows)])])[0]

    def arrive(round_of):
        for n, (dx, dy) in enumerate(SIDES):
            @pl.when(there(-dx, -dy))
            def _():
                all_of(round_of, n).wait_recv()

    def sent(round_of):
        for n, (dx, dy) in enumerate(SIDES):
            @pl.when(there(dx, dy))
            def _():
                all_of(round_of, n).wait_send()

    with phase("start1"):
        for c in sum_copies(member_sums, 0, members, next_member):
            c.start()
        start(first_round)

    with phase("w_msum"):
        sum_total(member_sums, 0, members).wait_recv()
    part = member_sums[0]
    for o in range(1, members):
        part = part + member_sums[o]
    group_sums[0] = part
    for c in sum_copies(group_sums, 2, groups, next_group):
        c.start()
    with phase("w_gsum"):
        sum_total(group_sums, 2, groups).wait_recv()
    with phase("mean"):
        total = group_sums[0]
        for o in range(1, groups):
            total = total + group_sums[o]
        mean = jnp.sum(total) / (cx * cy * cz * groups * members)
    with phase("w_halo1"):
        arrive(first_round)

    with phase("masks"):
        edge = lax.broadcasted_iota(jnp.int32, (8, cz), 0) < REACH
        for x in range(3):
            low, own, high = flags[x, 0], flags[x, 1], flags[x, 2]
            low, own, high = (jnp.broadcast_to(v[0:1], (8, cz)) for v in (low, own, high))
            active[x, pl.ds(0, 8), :] = jnp.where(edge, low, own)
            for t in range(1, window // 8 - 1):
                active[x, pl.ds(8 * t, 8), :] = own
            active[x, pl.ds(window - 8, 8), :] = jnp.where(edge, own, high)

    def lanes(value, step):
        lane = lax.broadcasted_iota(jnp.int32, value.shape, 1)
        low = jnp.where(lane < step, 0.0, pltpu.roll(value, step, 1))
        high = jnp.where(lane >= cz - step, 0.0, pltpu.roll(value, cz - step, 1))
        return low + high

    def neighbours(other, planes, row, rows, colour, mask, step):
        centres = {}
        out = []
        for p in planes:
            for q in (p - 1, p, p + 1):
                if q not in centres:
                    centres[q] = other[q, pl.ds(row, rows), :]
            near, far = (centres[p - 1], centres[p + 1]) if colour == 0 else (centres[p + 1], centres[p - 1])
            total = centres[p] + jnp.where(mask, near, far)
            total = total + (other[p, pl.ds(row - 1, rows), :] + other[p, pl.ds(row + 1, rows), :])
            out.append(total + lanes(centres[p], step))
        return out

    fine_mask = checker(window)

    def half_sweep(t, right, old, other, out, also=None):
        colour = t % 2
        wide_by = (REACH - t + 1) // 2
        rows = pl.ds(ROW0 - REACH, window)
        for region, low, high in ((0, HALO - wide_by, HALO), (1, HALO, HALO + px), (2, HALO + px, HALO + px + wide_by)):
            keep = active[region] > 0.5
            for first in range(low, high, 4):
                planes = range(first, min(first + 4, high))
                sums = neighbours(other, planes, ROW0 - REACH, window, colour, fine_mask, 1)
                for p, nbr in zip(planes, sums):
                    total = right[p, rows, :] - mean + nbr
                    before = old[p, rows, :]
                    out[p, rows, :] = jnp.where(keep, total * SIXTH, before)
                    if also is not None and region == 1:
                        also[p - HALO] = jnp.where(keep, 0.0, total - 6.0 * before)

    with phase("pre"):
        half_sweep(0, mix, mix, black, red)
        half_sweep(1, black_rhs, black, red, mid)
        half_sweep(2, mix, mix, mid, red)
        half_sweep(3, black_rhs, black, red, mid, defect)

    own_mask = checker(cy)

    def red_defects(other, planes):
        sums = neighbours(other, [HALO + a for a in planes], ROW0, cy, 0, own_mask, 1)
        for a, nbr in zip(planes, sums):
            centre = red[HALO + a, own_rows, :]
            yield a, centre, own_rhs[a] - mean + nbr - 6.0 * centre

    with phase("restrict"):
        even = wide_mask(cy)
        mixing = checker(hy, 0, 2) ^ jnp.logical_not(wide_mask(hy))
        for first in range(0, px, 4):
            for a, centre, res in red_defects(mid, range(first, first + 4)):
                both = res + defect[a, pl.ds(REACH, cy), :]
                pair_rows[a] = both + jnp.where(even, pltpu.roll(both, cz - 1, 1), pltpu.roll(both, 1, 1))
        for a in range(hx):
            first, second = (
                0.5 * (pair_rows[2 * a + k, pl.ds(0, hy, stride=2), :] + pair_rows[2 * a + k, pl.ds(1, hy, stride=2), :])
                for k in range(2)
            )
            mixed[CPLANE0 + a, pl.ds(CROW0, hy), :] = jnp.where(mixing, first, second)

    with phase("start2"):
        start(second_coarse)
        start(second_fine)
    with phase("w_coarse"):
        arrive(second_coarse)

    with phase("coarse"):
        coarse_rows = pl.ds(CROW0 - 8, cwindow)
        coarse_even = wide_mask(cwindow)
        coarse_mask = checker(cwindow, 0, 2)

        def regions(wide_by):
            first, last = CPLANE0, CPLANE0 + hx
            return (0, first - wide_by, first), (1, first, last), (2, last, last + wide_by)

        for region, low, high in regions(COARSE_HALO):
            weight = inside[region]
            for a in range(low, high):
                both = mixed[a, coarse_rows, :]
                s0 = jnp.where(coarse_even, both, pltpu.roll(both, 1, 1))
                rhs0[a, coarse_rows, :] = s0
                rhs1[a, coarse_rows, :] = jnp.where(coarse_even, pltpu.roll(both, cz - 1, 1), both)
                corr0[a, coarse_rows, :] = s0 * weight
        for t in range(1, 2 * COARSE):
            right, other, out = (rhs1, corr0, corr1) if t % 2 else (rhs0, corr1, corr0)
            for region, low, high in regions((COARSE_REACH - t + 1) // 2):
                weight = inside[region]
                for first in range(low, high, 4):
                    planes = range(first, min(first + 4, high))
                    sums = neighbours(other, planes, CROW0 - 8, cwindow, t % 2, coarse_mask, 2)
                    for a, nbr in zip(planes, sums):
                        out[a, coarse_rows, :] = (right[a, coarse_rows, :] + nbr) * weight

    with phase("w_fine2"):
        arrive(second_fine)
        sent(first_round)

    with phase("prolong"):
        half_rows = hy + 8
        rows = pl.ds(CROW0 - 4, half_rows)
        pick = checker(half_rows, 0, 2)
        low_rows, high_rows = pl.ds(ROW0 - 8, 8), pl.ds(ROW0 + cy, 8)
        sub = lax.broadcasted_iota(jnp.int32, (8, cz), 0)
        for p in range(px + 2 * HALO):
            a, k = CPLANE0 + (p - HALO) // 2, (p - HALO) % 2
            c0, c1 = corr0[a, rows, :], corr1[a, rows, :]
            plane = jnp.where(pick, c1, c0) if k else jnp.where(pick, c0, c1)
            wide[p, pl.ds(0, half_rows, stride=2), :] = plane
            wide[p, pl.ds(1, half_rows, stride=2), :] = plane
        for p in range(px + 2 * HALO):
            low, own, high = wide[p, pl.ds(0, 8), :], wide[p, pl.ds(8, cy), :], wide[p, pl.ds(8 + cy, 8), :]
            if HALO <= p < HALO + px:
                black[p, own_rows, :] = mid[p, own_rows, :] + own
                black[p, low_rows, :] = jnp.where(sub == 7, mid[p, low_rows, :], landed[p, low_rows, :]) + low
                black[p, high_rows, :] = jnp.where(sub == 0, mid[p, high_rows, :], landed[p, high_rows, :]) + high
            else:
                black[p, own_rows, :] = landed[p, own_rows, :] + own
                black[p, low_rows, :] = landed[p, low_rows, :] + low
                black[p, high_rows, :] = landed[p, high_rows, :] + high
            if 1 <= p < px + 2 * HALO - 1:
                red[p, own_rows, :] = red[p, own_rows, :] + own
                red[p, low_rows, :] = red[p, low_rows, :] + low
                red[p, high_rows, :] = red[p, high_rows, :] + high

    with phase("post"):
        half_sweep(0, mix, red, black, red)
        half_sweep(1, black_rhs, black, red, black)
        half_sweep(2, mix, red, black, red)
        half_sweep(3, black_rhs, black, red, black, defect)

    with phase("last"):
        for first in range(0, px, 4):
            for a, centre, res in red_defects(black, range(first, first + 4)):
                value = black[HALO + a, own_rows, :]
                other = defect[a, pl.ds(REACH, cy), :]
                smoothed_ref[2 * a] = jnp.where(own_mask, centre, value)
                smoothed_ref[2 * a + 1] = jnp.where(own_mask, value, centre)
                residual_ref[2 * a] = jnp.where(own_mask, res, other)
                residual_ref[2 * a + 1] = jnp.where(own_mask, other, res)

    with phase("w_sent"):
        sent(second_coarse)
        sent(second_fine)
        sum_total(member_sums, 0, members).wait_send()
        sum_total(group_sums, 2, groups).wait_send()


def put(smoothed, residual, smoothed_out, residual_out, sem):
    copies = [
        pltpu.make_async_copy(smoothed, smoothed_out, sem.at[0]),
        pltpu.make_async_copy(residual, residual_out, sem.at[1]),
    ]
    for c in copies:
        c.start()
    for c in copies:
        c.wait()


def per_device(dims, source, potential, refined):
    cx, cy, cz = source.shape
    groups, members = dims
    px, hx, hy = cx // 2, cx // 4, cy // 2
    fine = (px + 2 * HALO, ROW0 + cy + ROW0, cz)
    coarse = (hx + 2 * CPLANE0, hy + 2 * CROW0, cz)
    f32 = jnp.float32
    dma = pltpu.SemaphoreType.DMA
    any_spec = pl.BlockSpec(memory_space=pl.ANY)
    vmem_spec = pl.BlockSpec(memory_space=pltpu.VMEM)
    most = max((2 * HALO + 1) * cy, (3 * REACH) * px) + 8
    results = pl.pallas_call(
        functools.partial(kernel, dims, (cx, cy, cz)),
        out_shape=[pltpu.VMEM(source.shape, f32)] * 2,
        in_specs=[pl.BlockSpec(memory_space=pltpu.SMEM), any_spec, any_spec],
        out_specs=[vmem_spec] * 2,
        scratch_shapes=[
            pltpu.VMEM((2, cx, cy, cz), f32),
            pltpu.VMEM((3, *fine), f32),
            pltpu.VMEM((px, cy, cz), f32),
            pltpu.VMEM(fine, f32),
            pltpu.VMEM(fine, f32),
            pltpu.VMEM(fine, f32),
            pltpu.VMEM((px, cy + 2 * REACH, cz), f32),
            pltpu.VMEM((px, cy, cz), f32),
            pltpu.VMEM(coarse, f32),
            pltpu.VMEM(coarse, f32),
            pltpu.VMEM(coarse, f32),
            pltpu.VMEM(coarse, f32),
            pltpu.VMEM(coarse, f32),
            pltpu.VMEM((px + 2 * HALO, cy + 16, cz), f32),
            pltpu.VMEM((3, 3, 8, cz), f32),
            pltpu.VMEM((3, cy + 2 * REACH, cz), f32),
            pltpu.VMEM((3, hy + 16, cz), f32),
            pltpu.VMEM((members, 8, cz), f32),
            pltpu.VMEM((groups, 8, cz), f32),
            pltpu.VMEM((most, cz), f32),
            dma((2,)),
            dma((3, len(SIDES))),
            dma((3, len(SIDES))),
            dma((4,)),
        ],
        compiler_params=pltpu.CompilerParams(collective_id=0, has_side_effects=True),
    )(refined, source, potential)
    return tuple(pl.pallas_call(
        put,
        out_shape=[jax.ShapeDtypeStruct(source.shape, f32)] * 2,
        in_specs=[any_spec] * 2,
        out_specs=[any_spec] * 2,
        scratch_shapes=[dma((2,))],
    )(*(pltpu.with_memory_space_constraint(v, pltpu.VMEM) for v in results)))


def solution(mesh):
    spec = P("group", "member", None)
    return jax.shard_map(
        functools.partial(per_device, (mesh.shape["group"], mesh.shape["member"])),
        mesh=mesh,
        in_specs=(spec, spec, spec),
        out_specs=(spec, spec),
        check_vma=False,
    )
```

time: 38.2 us -> 23.2 us (0.61)
  Pallas kernels: 34.7 us -> 22.4 us
  local copies, waits for them, and re-layouts: 2.72 us -> 0 us
    pallas_call x1, Pallas kernels: 34.7 us -> 21.4 us  [per_device(): pl.pallas_call(functools.partial(kernel, dims, (cx, cy, cz)), out_shape=[...]
    unnamed x4 -> x0, local copies, waits for them, and re-layouts: 2.72 us -> none
    pallas_call x0 -> x1, Pallas kernels: none -> 0.99 us  [per_device(): pl.pallas_call(put, out_shape=[jax.ShapeDtypeStruct(source.shape, f32)] *...]
where the time goes in v1:
time: 23.2 us; the launch traced here: 23.1 us
  Pallas kernels  22.4 us (97%)
  between operations  0.64 us (3%)
    pallas_call x1, Pallas kernels, per_device(): pl.pallas_call(functools.partial(kernel, dims, (cx, cy, cz)), out_shape=[...  21.4 us
    pallas_call x1, Pallas kernels, per_device(): pl.pallas_call(put, out_shape=[jax.ShapeDtypeStruct(source.shape, f32)] *...  0.99 us

profile of v1, /device:TPU:0, one launch (start us, length us, event | category | flops | bytes accessed | tf_op | source)
XLA Modules:
  0.0 23.1 jit_solution(3769627426709185961)
XLA Ops:
  0.6 21.4 %shard_map.50 = (f32[32,32,128]{2,1,0:T(8,128)S(1)}, f32[32,32,128]{2,1,0:T(8,128)S(1)}) custom-call(s32[1,1,4]{2,1,0:T(1,128)} %refined_ref.1, f32[32,32,128]{2,1,0:T(8,128)} %source_ref.1, f32[32,32,128]{2,1,0:T(8,128)} %potential_ref.1), custom_call_target="tpu_custom_call" | custom-call | tf_op jit(solution)/shard_map/pallas_call | solution.py:471
  22.1 1.0 %shard_map.51 = (f32[32,32,128]{2,1,0:T(8,128)}, f32[32,32,128]{2,1,0:T(8,128)}) custom-call(f32[32,32,128]{2,1,0:T(8,128)S(1)} %get-tuple-element.4.smoothed, f32[32,32,128]{2,1,0:T(8,128)S(1)} %get-tuple-element.5.residual), custom_call_target="tpu_custom_call" | custom-call | tf_op jit(solution)/shard_map/pallas_call | solution.py:504

commit v2 on v1

v2 whole, which is shorter than its diff:
```python
import contextlib
import functools

import jax
import jax.numpy as jnp
from jax import lax
from jax.experimental import pallas as pl
from jax.experimental.pallas import tpu as pltpu
from jax.sharding import PartitionSpec as P

SWEEPS = 2
COARSE = 2
REACH = 2 * SWEEPS
HALO = (REACH + 2) // 2
COARSE_REACH = 2 * COARSE - 1 + (REACH + 2) // 2
COARSE_HALO = COARSE_REACH // 2
ROW0 = 8 + REACH
CROW0 = 16
CPLANE0 = COARSE_HALO + 1
SIDES = ((0, -1), (0, 1), (-1, 0), (1, 0), (-1, -1), (-1, 1), (1, -1), (1, 1))
MESH = pl.DeviceIdType.MESH
SIXTH = 1.0 / 6.0
PIECES = 4


def phase(name):
    return contextlib.nullcontext()


def span(side, begin, end, first, count):
    if side == 0:
        return pl.ds(first, count), pl.ds(first, count)
    if side > 0:
        return pl.ds(first + count - end, end - begin), pl.ds(first - end, end - begin)
    return pl.ds(first + begin, end - begin), pl.ds(first + count + begin, end - begin)


def checker(rows, cz, lanes_per=1):
    r = lax.broadcasted_iota(jnp.int32, (rows, cz), 0)
    return ((r + lax.broadcasted_iota(jnp.int32, (rows, cz), 1) // lanes_per) & 1) == 0


def lanes(value, step):
    cz = value.shape[1]
    lane = lax.broadcasted_iota(jnp.int32, value.shape, 1)
    low = jnp.where(lane < step, 0.0, pltpu.roll(value, step, 1))
    high = jnp.where(lane >= cz - step, 0.0, pltpu.roll(value, cz - step, 1))
    return low + high


def neighbours(other, planes, row, rows, colour, mask, step):
    centres = {}
    out = []
    for p in planes:
        for q in (p - 1, p, p + 1):
            if q not in centres:
                centres[q] = other[q, pl.ds(row, rows), :]
        near, far = (centres[p - 1], centres[p + 1]) if colour == 0 else (centres[p + 1], centres[p - 1])
        total = centres[p] + jnp.where(mask, near, far)
        total = total + (other[p, pl.ds(row - 1, rows), :] + other[p, pl.ds(row + 1, rows), :])
        out.append(total + lanes(centres[p], step))
    return out


def kernel(
    dims, sizes,
    refined_hbm, source_ref, potential_ref,
    red, post, defect, own_rhs,
    refined_ref, raw, field, mid, landed, pair_rows, mixed, rhs0, rhs1, corr0, corr1, wide,
    flags, active, inside, member_sums, group_sums, zeros, dummy,
    local_sem, send_sem, recv_sem, sum_sem,
):
    groups, members = dims
    cx, cy, cz = sizes
    px, hx, hy = cx // 2, cx // 4, cy // 2
    group_at = lax.axis_index("group")
    member_at = lax.axis_index("member")
    f32 = jnp.float32
    black, mix, black_rhs = field.at[0], field.at[1], field.at[2]
    own_rows = pl.ds(ROW0, cy)
    window = cy + 2 * REACH
    cwindow = hy + 16

    load_source = pltpu.make_async_copy(source_ref, raw.at[0], local_sem.at[0])
    load_potential = pltpu.make_async_copy(potential_ref, raw.at[1], local_sem.at[1])
    load_refined = pltpu.make_async_copy(refined_hbm, refined_ref, local_sem.at[2])
    load_source.start()
    load_potential.start()
    load_refined.start()

    def there(dx, dy):
        ok = None
        for side, at, count in ((dx, group_at, groups), (dy, member_at, members)):
            if side == 0:
                continue
            here = at > 0 if side < 0 else at < count - 1
            ok = here if ok is None else ok & here
        return ok

    def device(dx, dy):
        return (group_at + dx, member_at + dy)

    barrier = pltpu.get_barrier_semaphore()
    for o in range(1, members):
        pl.semaphore_signal(barrier, inc=1, device_id=(group_at, lax.rem(member_at + o, members)), device_id_type=MESH)
    for o in range(1, groups):
        pl.semaphore_signal(barrier, inc=1, device_id=(lax.rem(group_at + o, groups), member_at), device_id_type=MESH)
    expected = jnp.int32(groups - 1 + members - 1)
    for dx, dy in SIDES:
        if dx and dy:
            @pl.when(there(dx, dy))
            def _():
                pl.semaphore_signal(barrier, inc=1, device_id=device(dx, dy), device_id_type=MESH)
            expected = expected + there(dx, dy).astype(jnp.int32)

    blank_rows = jnp.zeros((cy, cz), f32)
    for kind in range(2):
        for p in range(px):
            zeros[kind, p] = blank_rows
    blank_coarse = jnp.zeros((cwindow, cz), f32)
    for a in range(hx + 2 * CPLANE0):
        mixed[a, pl.ds(CROW0 - 8, cwindow), :] = blank_coarse
    for a in (0, hx + 2 * CPLANE0 - 1):
        corr0[a, pl.ds(CROW0 - 8, cwindow), :] = blank_coarse

    crow = lax.broadcasted_iota(jnp.int32, (cwindow, cz), 0) - 8
    clow = jnp.where(member_at > 0, -8, 0)
    chigh = jnp.where(member_at < members - 1, hy + 8, hy)
    within = jnp.where((crow >= clow) & (crow < chigh), SIXTH, 0.0)
    for region in range(3):
        alive = 1.0 if region == 1 else there(region - 1, 0).astype(f32)
        inside[region] = within * alive

    def wide_mask(rows):
        return lax.broadcasted_iota(jnp.int32, (rows, cz), 1) % 2 == 0

    with phase("load"):
        load_refined.wait()
        lane1 = lax.broadcasted_iota(jnp.int32, (1, cz), 1)
        boxes = refined_ref.shape[2]
        box = cz // boxes
        marks = jnp.zeros((1, cz), jnp.int32)
        for b in range(boxes):
            marks = jnp.where(lane1 // box == b, jnp.full((1, cz), refined_ref[0, 0, b], jnp.int32), marks)
        flags[1, 1, pl.ds(0, 1), :] = (marks == 1).astype(f32)
        load_source.wait()
        load_potential.wait()

    with phase("pack"):
        here = checker(cy, cz)
        smooth_own = jnp.broadcast_to(flags[1, 1, 0:1, :], (cy, cz)) > 0.5
        acc = [jnp.zeros((8, cz), f32)] * 4
        for a in range(px):
            s0, s1 = raw[0, 2 * a], raw[0, 2 * a + 1]
            v0, v1 = raw[1, 2 * a], raw[1, 2 * a + 1]
            both = s0 + s1
            acc = [acc[t] + sum(both[8 * u:8 * u + 8] for u in range(t, cy // 8, 4)) for t in range(4)]
            red_rhs = jnp.where(here, s0, s1)
            own_rhs[a] = red_rhs
            mix[HALO + a, own_rows, :] = jnp.where(smooth_own, red_rhs, jnp.where(here, v0, v1))
            black[HALO + a, own_rows, :] = jnp.where(here, v1, v0)
            black_rhs[HALO + a, own_rows, :] = jnp.where(here, s1, s0)
        acc = (acc[0] + acc[1]) + (acc[2] + acc[3])
        member_sums[0, pl.ds(0, 1), :] = jnp.sum(acc, axis=0, keepdims=True)

    with phase("barrier"):
        pl.semaphore_wait(barrier, expected)

    row = pl.ds(0, 1)

    def sum_copies(slots, n, count, target):
        return [
            pltpu.make_async_remote_copy(
                src_ref=slots.at[0, row], dst_ref=slots.at[o, row], send_sem=sum_sem.at[n], recv_sem=sum_sem.at[n + 1],
                device_id=target(o), device_id_type=MESH,
            )
            for o in range(1, count)
        ]

    def sum_total(slots, n, count):
        others = slots.at[pl.ds(1, count - 1), row]
        return pltpu.make_async_remote_copy(
            src_ref=others, dst_ref=others, send_sem=sum_sem.at[n], recv_sem=sum_sem.at[n + 1],
            device_id=(group_at, member_at), device_id_type=MESH,
        )

    def next_member(o):
        return (group_at, lax.rem(member_at + o, members))

    def next_group(o):
        return (lax.rem(group_at + o, groups), member_at)

    def first_round(n):
        dx, dy = SIDES[n]
        pairs = [(flags.at[1, 1, row], flags.at[1 - dx, 1 - dy, row])]
        if dx and dy:
            pieces = ((0, 1, 0, 1, 4), (1, 1, 0, 1, 3), (2, 1, 0, 1, 2), (0, 1, 1, 2, 2), (1, 1, 1, 2, 1))
        elif dx:
            pieces = ((0, 1, 0, HALO, cy), (1, 2, 0, HALO - 1, cy))
        else:
            pieces = ((0, 1, 0, px, REACH + 1), (1, 1, 0, px, REACH), (2, 1, 0, px, REACH - 1))
        for kind, kinds, begin, end, deep in pieces:
            sx, tx = span(dx, begin, end, HALO, px)
            sy, ty = span(dy, 0, deep, ROW0, cy)
            pairs.append((field.at[pl.ds(kind, kinds), sx, sy], field.at[pl.ds(kind, kinds), tx, ty]))
        return 0, pairs

    def second_coarse(n):
        dx, dy = SIDES[n]
        if dx and dy:
            pieces = ((0, 1, 5), (1, 2, 3), (2, 3, 1))
        elif dx:
            pieces = ((0, COARSE_HALO, hy),)
        else:
            pieces = ((0, hx, COARSE_REACH),)
        pairs = []
        for begin, end, deep in pieces:
            sx, tx = span(dx, begin, end, CPLANE0, hx)
            sy, ty = span(dy, 0, deep, CROW0, hy)
            pairs.append((mixed.at[sx, sy], mixed.at[tx, ty]))
        return 1, pairs

    def second_fine(n, early):
        dx, dy = SIDES[n]
        if dx and dy:
            pieces = () if early else ((0, 1, 0, 4), (1, 2, 0, 2))
        elif dx:
            pieces = () if early else ((0, HALO, 0, cy),)
        else:
            pieces = ((0, px // 2, 1, REACH + 1),) if early else ((px // 2, px, 1, REACH + 1),)
        pairs = []
        for begin, end, skip, deep in pieces:
            if dx:
                sx, tx = span(dx, begin, end, HALO, px)
            else:
                sx = tx = pl.ds(HALO + begin, end - begin)
            sy, ty = span(dy, skip, deep, ROW0, cy)
            pairs.append((mid.at[sx, sy], landed.at[tx, ty]))
        return 2, pairs

    early_fine = functools.partial(second_fine, early=True)
    late_fine = functools.partial(second_fine, early=False)

    def rows_of(pairs):
        total = 0
        for _, dst in pairs:
            total += functools.reduce(lambda p, q: p * q, dst.shape[:-1])
        return total

    def start(round_of):
        for n, (dx, dy) in enumerate(SIDES):
            kind, pairs = round_of(n)
            if not pairs:
                continue

            @pl.when(there(dx, dy))
            def _():
                for src, dst in pairs:
                    pltpu.make_async_remote_copy(
                        src_ref=src, dst_ref=dst, send_sem=send_sem.at[n], recv_sem=recv_sem.at[kind],
                        device_id=device(dx, dy), device_id_type=MESH,
                    ).start()

    def fill(round_of):
        for n, (dx, dy) in enumerate(SIDES):
            kind, pairs = round_of(n)
            if not pairs:
                continue

            @pl.when(jnp.logical_not(there(-dx, -dy)))
            def _():
                for _, dst in pairs:
                    shape = dst.shape[:-1]
                    src = zeros.at[(0,) * (4 - len(dst.shape)) + tuple(pl.ds(0, size) for size in shape)]
                    pltpu.make_async_copy(src, dst, recv_sem.at[kind]).start()

    def all_of(rows, n, kind):
        part = dummy.at[pl.ds(0, rows)]
        return pltpu.make_async_remote_copy(
            src_ref=part, dst_ref=part, send_sem=send_sem.at[n], recv_sem=recv_sem.at[kind],
            device_id=(group_at, member_at), device_id_type=MESH,
        )

    def arrive(*rounds):
        rows, kind = 0, None
        for round_of in rounds:
            for n in range(len(SIDES)):
                kind, pairs = round_of(n)
                rows += rows_of(pairs)
        all_of(rows, 0, kind).wait_recv()

    def sent(*rounds):
        for n, (dx, dy) in enumerate(SIDES):
            rows = sum(rows_of(round_of(n)[1]) for round_of in rounds)

            @pl.when(there(dx, dy))
            def _():
                all_of(rows, n, 0).wait_send()

    with phase("start1"):
        for c in sum_copies(member_sums, 0, members, next_member):
            c.start()
        start(first_round)
        fill(first_round)
        fill(second_coarse)
        fill(early_fine)
        fill(late_fine)

    with phase("w_msum"):
        sum_total(member_sums, 0, members).wait_recv()
    part = member_sums[0, row, :]
    for o in range(1, members):
        part = part + member_sums[o, row, :]
    group_sums[0, row, :] = part
    for c in sum_copies(group_sums, 2, groups, next_group):
        c.start()
    with phase("w_gsum"):
        sum_total(group_sums, 2, groups).wait_recv()
    with phase("mean"):
        total = group_sums[0, row, :]
        for o in range(1, groups):
            total = total + group_sums[o, row, :]
        mean = jnp.sum(total) / (cx * cy * cz * groups * members)
    with phase("w_halo1"):
        arrive(first_round)

    with phase("masks"):
        edge = lax.broadcasted_iota(jnp.int32, (8, cz), 0) < REACH
        for x in range(3):
            low, own, high = flags[x, 0], flags[x, 1], flags[x, 2]
            low, own, high = (jnp.broadcast_to(v[0:1], (8, cz)) for v in (low, own, high))
            active[x, pl.ds(0, 8), :] = jnp.where(edge, low, own)
            for t in range(1, window // 8 - 1):
                active[x, pl.ds(8 * t, 8), :] = own
            active[x, pl.ds(window - 8, 8), :] = jnp.where(edge, own, high)

    fine_mask = checker(window, cz)

    def half_sweep(t, right, old, other, out, also=None):
        colour = t % 2
        wide_by = (REACH - t + 1) // 2
        rows = pl.ds(ROW0 - REACH, window)
        for region, low, high in ((0, HALO - wide_by, HALO), (1, HALO, HALO + px), (2, HALO + px, HALO + px + wide_by)):
            keep = active[region] > 0.5
            for first in range(low, high, 4):
                planes = range(first, min(first + 4, high))
                sums = neighbours(other, planes, ROW0 - REACH, window, colour, fine_mask, 1)
                for p, nbr in zip(planes, sums):
                    total = right[p, rows, :] - mean + nbr
                    before = old[p, rows, :]
                    out[p, rows, :] = jnp.where(keep, total * SIXTH, before)
                    if also is not None and region == 1:
                        also[p - HALO] = jnp.where(keep, 0.0, total - 6.0 * before)

    with phase("pre"):
        half_sweep(0, mix, mix, black, red)
        half_sweep(1, black_rhs, black, red, mid)
        half_sweep(2, mix, mix, mid, red)
        half_sweep(3, black_rhs, black, red, mid, defect)

    own_mask = checker(cy, cz)

    def red_defects(other, planes):
        sums = neighbours(other, [HALO + a for a in planes], ROW0, cy, 0, own_mask, 1)
        for a, nbr in zip(planes, sums):
            centre = red[HALO + a, own_rows, :]
            yield a, centre, own_rhs[a] - mean + nbr - 6.0 * centre

    with phase("start_early"):
        start(early_fine)

    with phase("restrict"):
        for first in range(0, px, 4):
            for a, centre, res in red_defects(mid, range(first, first + 4)):
                pair_rows[a] = res + defect[a, pl.ds(REACH, cy), :]
        chosen, even = checker(hy, cz, 2), wide_mask(hy)
        for a in range(hx):
            first, second = (
                pair_rows[2 * a + k, pl.ds(0, hy, stride=2), :] + pair_rows[2 * a + k, pl.ds(1, hy, stride=2), :]
                for k in range(2)
            )
            zero, one = jnp.where(chosen, first, second), jnp.where(chosen, second, first)
            both = jnp.where(even, zero + pltpu.roll(zero, cz - 1, 1), one + pltpu.roll(one, 1, 1))
            mixed[CPLANE0 + a, pl.ds(CROW0, hy), :] = 0.5 * both

    with phase("start2"):
        start(second_coarse)
        start(late_fine)
        for a in range(px):
            own_rhs[a] = own_rhs[a] - mean
    with phase("w_coarse"):
        arrive(second_coarse)

    with phase("coarse"):
        coarse_rows = pl.ds(CROW0 - 8, cwindow)
        coarse_even = wide_mask(cwindow)
        coarse_mask = checker(cwindow, cz, 2)

        def regions(wide_by):
            first, last = CPLANE0, CPLANE0 + hx
            return (0, first - wide_by, first), (1, first, last), (2, last, last + wide_by)

        for region, low, high in regions(COARSE_HALO):
            weight = inside[region]
            for a in range(low, high):
                both = mixed[a, coarse_rows, :]
                s0 = jnp.where(coarse_even, both, pltpu.roll(both, 1, 1))
                rhs0[a, coarse_rows, :] = s0
                rhs1[a, coarse_rows, :] = jnp.where(coarse_even, pltpu.roll(both, cz - 1, 1), both)
                corr0[a, coarse_rows, :] = s0 * weight
        for t in range(1, 2 * COARSE):
            right, other, out = (rhs1, corr0, corr1) if t % 2 else (rhs0, corr1, corr0)
            for region, low, high in regions((COARSE_REACH - t + 1) // 2):
                weight = inside[region]
                for first in range(low, high, 4):
                    planes = range(first, min(first + 4, high))
                    sums = neighbours(other, planes, CROW0 - 8, cwindow, t % 2, coarse_mask, 2)
                    for a, nbr in zip(planes, sums):
                        out[a, coarse_rows, :] = (right[a, coarse_rows, :] + nbr) * weight

    with phase("w_fine2"):
        arrive(early_fine, late_fine)

    with phase("prolong"):
        half_rows = hy + 8
        rows = pl.ds(CROW0 - 4, half_rows)
        pick = checker(half_rows, cz, 2)
        low_rows, high_rows = pl.ds(ROW0 - 8, 8), pl.ds(ROW0 + cy, 8)
        sub = lax.broadcasted_iota(jnp.int32, (8, cz), 0)
        for p in range(px + 2 * HALO):
            a, k = CPLANE0 + (p - HALO) // 2, (p - HALO) % 2
            c0, c1 = corr0[a, rows, :], corr1[a, rows, :]
            plane = jnp.where(pick, c1, c0) if k else jnp.where(pick, c0, c1)
            wide[p, pl.ds(0, half_rows, stride=2), :] = plane
            wide[p, pl.ds(1, half_rows, stride=2), :] = plane
        for p in range(px + 2 * HALO):
            low, own, high = wide[p, pl.ds(0, 8), :], wide[p, pl.ds(8, cy), :], wide[p, pl.ds(8 + cy, 8), :]
            if HALO <= p < HALO + px:
                post[p, own_rows, :] = mid[p, own_rows, :] + own
                post[p, low_rows, :] = jnp.where(sub == 7, mid[p, low_rows, :], landed[p, low_rows, :]) + low
                post[p, high_rows, :] = jnp.where(sub == 0, mid[p, high_rows, :], landed[p, high_rows, :]) + high
            else:
                post[p, own_rows, :] = landed[p, own_rows, :] + own
                post[p, low_rows, :] = landed[p, low_rows, :] + low
                post[p, high_rows, :] = landed[p, high_rows, :] + high
            if 1 <= p < px + 2 * HALO - 1:
                red[p, own_rows, :] = red[p, own_rows, :] + own
                red[p, low_rows, :] = red[p, low_rows, :] + low
                red[p, high_rows, :] = red[p, high_rows, :] + high

    with phase("post"):
        half_sweep(0, mix, red, post, red)
        half_sweep(1, black_rhs, post, red, post)
        half_sweep(2, mix, red, post, red)
        half_sweep(3, black_rhs, post, red, post, defect)

    with phase("w_sent"):
        sent(first_round, second_coarse, early_fine, late_fine)
        sum_total(member_sums, 0, members).wait_send()
        sum_total(group_sums, 2, groups).wait_send()


def put(red, post, defect, contrast, smoothed_out, residual_out, smoothed, residual, sem):
    px, cy, cz = contrast.shape
    own_rows = pl.ds(ROW0, cy)
    mask = checker(cy, cz)
    size = px // PIECES
    copies = []
    for piece in range(PIECES):
        planes = range(piece * size, (piece + 1) * size)
        part = pl.ds(2 * piece * size, 2 * size)
        for a in planes:
            centre, value = red[HALO + a, own_rows, :], post[HALO + a, own_rows, :]
            smoothed[2 * a] = jnp.where(mask, centre, value)
            smoothed[2 * a + 1] = jnp.where(mask, value, centre)
        copies.append(pltpu.make_async_copy(smoothed.at[part], smoothed_out.at[part], sem.at[0, piece]))
        copies[-1].start()
        sums = neighbours(post, [HALO + a for a in planes], ROW0, cy, 0, mask, 1)
        for a, nbr in zip(planes, sums):
            res, other = contrast[a] + nbr - 6.0 * red[HALO + a, own_rows, :], defect[a, pl.ds(REACH, cy), :]
            residual[2 * a] = jnp.where(mask, res, other)
            residual[2 * a + 1] = jnp.where(mask, other, res)
        copies.append(pltpu.make_async_copy(residual.at[part], residual_out.at[part], sem.at[1, piece]))
        copies[-1].start()
    for c in copies:
        c.wait()


def per_device(dims, source, potential, refined):
    cx, cy, cz = source.shape
    groups, members = dims
    px, hx, hy = cx // 2, cx // 4, cy // 2
    fine = (px + 2 * HALO, ROW0 + cy + ROW0, cz)
    coarse = (hx + 2 * CPLANE0, hy + 2 * CROW0, cz)
    f32 = jnp.float32
    dma = pltpu.SemaphoreType.DMA
    any_spec = pl.BlockSpec(memory_space=pl.ANY)
    vmem_spec = pl.BlockSpec(memory_space=pltpu.VMEM)
    results = pl.pallas_call(
        functools.partial(kernel, dims, (cx, cy, cz)),
        out_shape=[
            pltpu.VMEM(fine, f32),
            pltpu.VMEM(fine, f32),
            pltpu.VMEM((px, cy + 2 * REACH, cz), f32),
            pltpu.VMEM((px, cy, cz), f32),
        ],
        in_specs=[any_spec] * 3,
        out_specs=[vmem_spec] * 4,
        scratch_shapes=[
            pltpu.SMEM(refined.shape, jnp.int32),
            pltpu.VMEM((2, cx, cy, cz), f32),
            pltpu.VMEM((3, *fine), f32),
            pltpu.VMEM(fine, f32),
            pltpu.VMEM(fine, f32),
            pltpu.VMEM((px, cy, cz), f32),
            pltpu.VMEM(coarse, f32),
            pltpu.VMEM(coarse, f32),
            pltpu.VMEM(coarse, f32),
            pltpu.VMEM(coarse, f32),
            pltpu.VMEM(coarse, f32),
            pltpu.VMEM((px + 2 * HALO, cy + 16, cz), f32),
            pltpu.VMEM((3, 3, 8, cz), f32),
            pltpu.VMEM((3, cy + 2 * REACH, cz), f32),
            pltpu.VMEM((3, hy + 16, cz), f32),
            pltpu.VMEM((members, 8, cz), f32),
            pltpu.VMEM((groups, 8, cz), f32),
            pltpu.VMEM((2, px, cy, cz), f32),
            pltpu.VMEM((64 * cy, cz), f32),
            dma((3,)),
            dma((len(SIDES),)),
            dma((3,)),
            dma((4,)),
        ],
        compiler_params=pltpu.CompilerParams(collective_id=0, has_side_effects=True),
    )(refined, source, potential)
    return tuple(pl.pallas_call(
        put,
        out_shape=[jax.ShapeDtypeStruct(source.shape, f32)] * 2,
        in_specs=[vmem_spec] * 4,
        out_specs=[any_spec] * 2,
        scratch_shapes=[pltpu.VMEM(source.shape, f32), pltpu.VMEM(source.shape, f32), dma((2, PIECES))],
    )(*(pltpu.with_memory_space_constraint(v, pltpu.VMEM) for v in results)))


def solution(mesh):
    spec = P("group", "member", None)
    return jax.shard_map(
        functools.partial(per_device, (mesh.shape["group"], mesh.shape["member"])),
        mesh=mesh,
        in_specs=(spec, spec, spec),
        out_specs=(spec, spec),
        check_vma=False,
    )
```

time: 23.2 us -> 21.2 us (0.914)
  Pallas kernels: 22.4 us -> 20.4 us
    pallas_call x1, Pallas kernels: 21.4 us -> 19.3 us  [per_device(): pl.pallas_call(functools.partial(kernel, dims, (cx, cy, cz)), out_shape=[...]
where the time goes in v2:
time: 21.2 us; the launch traced here: 21.1 us
  Pallas kernels  20.4 us (96%)
  between operations  0.64 us (3%)
    pallas_call x1, Pallas kernels, per_device(): pl.pallas_call(functools.partial(kernel, dims, (cx, cy, cz)), out_shape=[...  19.3 us
    pallas_call x1, Pallas kernels, per_device(): pl.pallas_call(put, out_shape=[jax.ShapeDtypeStruct(source.shape, f32)] *...  1.11 us

profile of v2, /device:TPU:0, one launch (start us, length us, event | category | flops | bytes accessed | tf_op | source)
XLA Modules:
  0.0 21.1 jit_solution(3019706589370511045)
XLA Ops:
  0.6 19.3 %shard_map.50 = (f32[22,56,128]{2,1,0:T(8,128)S(1)}, f32[22,56,128]{2,1,0:T(8,128)S(1)}, f32[16,40,128]{2,1,0:T(8,128)S(1)}, f32[16,32,128]{2,1,0:T(8,128)S(1)}) custom-call(s32[1,1,4]{2,1,0:T(1,128)} %refined_hbm.1, f32[32,32,128]{2,1,0:T(8,128)} %source_ref.1, f32[32,32,128]{2,1,0:T(8,128)} %potential_ref.1), custom_call_target="tpu_custom_call" | custom-call | tf_op jit(solution)/shard_map/pallas_call | solution.py:499
  19.9 1.1 %shard_map.51 = (f32[32,32,128]{2,1,0:T(8,128)}, f32[32,32,128]{2,1,0:T(8,128)}) custom-call(f32[22,56,128]{2,1,0:T(8,128)S(1)} %get-tuple-element.6.red, f32[22,56,128]{2,1,0:T(8,128)S(1)} %get-tuple-element.7.post, f32[16,40,128]{2,1,0:T(8,128)S(1)} %get-tuple-element.8.defect, f32[16,32,128]{2,1,0:T(8,128)S(1)} %get-tuple-element.9.contrast), custom_call_target="tpu_custom_call" | custom-call | tf_op jit(solution)/shard_map/pallas_call | solution.py:536

commit v3 on v2

--- a/solution.py
+++ b/solution.py
@@ -67,8 +67,8 @@
     refined_hbm, source_ref, potential_ref,
     red, post, defect, own_rhs,
     refined_ref, raw, field, mid, landed, pair_rows, mixed, rhs0, rhs1, corr0, corr1, wide,
-    flags, active, inside, member_sums, group_sums, zeros, dummy,
-    local_sem, send_sem, recv_sem, sum_sem,
+    flags, active, inside, member_sums, group_sums, direct, zeros, dummy,
+    local_sem, send_sem, recv_sem, sum_sem, ready,
 ):
     groups, members = dims
     cx, cy, cz = sizes
@@ -100,18 +100,25 @@
     def device(dx, dy):
         return (group_at + dx, member_at + dy)
 
+    def signal(sem, at):
+        pl.semaphore_signal(sem, inc=1, device_id=at, device_id_type=MESH)
+
     barrier = pltpu.get_barrier_semaphore()
     for o in range(1, members):
-        pl.semaphore_signal(barrier, inc=1, device_id=(group_at, lax.rem(member_at + o, members)), device_id_type=MESH)
-    for o in range(1, groups):
-        pl.semaphore_signal(barrier, inc=1, device_id=(lax.rem(group_at + o, groups), member_at), device_id_type=MESH)
-    expected = jnp.int32(groups - 1 + members - 1)
-    for dx, dy in SIDES:
-        if dx and dy:
-            @pl.when(there(dx, dy))
-            def _():
-                pl.semaphore_signal(barrier, inc=1, device_id=device(dx, dy), device_id_type=MESH)
-            expected = expected + there(dx, dy).astype(jnp.int32)
+        signal(barrier, (group_at, lax.rem(member_at + o, members)))
+    expected = jnp.int32(members - 1) + group_at * members
+    for dy in (-1, 0, 1):
+        @pl.when(there(-1, dy))
+        def _():
+            signal(barrier, device(-1, dy))
+        expected = expected + there(1, dy).astype(jnp.int32)
+
+    def greet(o, carry):
+        for m in range(members):
+            signal(barrier, (group_at + o, m))
+        return carry
+
+    lax.fori_loop(1, groups - group_at, greet, 0)
 
     blank_rows = jnp.zeros((cy, cz), f32)
     for kind in range(2):
@@ -166,29 +173,55 @@
     with phase("barrier"):
         pl.semaphore_wait(barrier, expected)
 
+    def report(g, carry):
+        signal(ready, (g, member_at))
+        return carry
+
     row = pl.ds(0, 1)
 
-    def sum_copies(slots, n, count, target):
-        return [
-            pltpu.make_async_remote_copy(
-                src_ref=slots.at[0, row], dst_ref=slots.at[o, row], send_sem=sum_sem.at[n], recv_sem=sum_sem.at[n + 1],
-                device_id=target(o), device_id_type=MESH,
-            )
-            for o in range(1, count)
-        ]
-
-    def sum_total(slots, n, count):
-        others = slots.at[pl.ds(1, count - 1), row]
+    def sum_copy(src, dst, n, at):
         return pltpu.make_async_remote_copy(
-            src_ref=others, dst_ref=others, send_sem=sum_sem.at[n], recv_sem=sum_sem.at[n + 1],
-            device_id=(group_at, member_at), device_id_type=MESH,
+            src_ref=src, dst_ref=dst, send_sem=sum_sem.at[n], recv_sem=sum_sem.at[n + 1], device_id=at, device_id_type=MESH,
         )
 
-    def next_member(o):
-        return (group_at, lax.rem(member_at + o, members))
-
-    def next_group(o):
-        return (lax.rem(group_at + o, groups), member_at)
+    own_sum, plane_sum = member_sums.at[0, row], group_sums.at[0, row]
+    no_sum = zeros.at[0, 0, row]
+
+    def share_in_plane():
+        for o in range(1, members):
+            sum_copy(own_sum, member_sums.at[o, row], 0, (group_at, lax.rem(member_at + o, members))).start()
+
+    def share_with_earlier():
+        for o in range(groups - 1, 0, -1):
+            @pl.when(group_at >= o)
+            def _():
+                for m in range(members):
+                    sum_copy(own_sum, direct.at[o, pl.ds(member_at, 1)], 2, (group_at - o, m)).start()
+
+    def fill_sums():
+        for o in range(1, groups):
+            @pl.when(group_at < o)
+            def _():
+                pltpu.make_async_copy(zeros.at[0, 0, pl.ds(0, members)], dummy.at[pl.ds(o * members, members)], sum_sem.at[2]).start()
+                pltpu.make_async_copy(no_sum, group_sums.at[o, row], sum_sem.at[5]).start()
+
+            @pl.when(group_at + o >= groups)
+            def _():
+                pltpu.make_async_copy(zeros.at[0, 0, pl.ds(0, members)], direct.at[o], sum_sem.at[3]).start()
+                pltpu.make_async_copy(no_sum, dummy.at[pl.ds(groups * members + o, 1)], sum_sem.at[4]).start()
+
+    def share_with_later():
+        for o in range(1, groups):
+            @pl.when(group_at + o < groups)
+            def _():
+                sum_copy(plane_sum, group_sums.at[o, row], 4, (group_at + o, member_at)).start()
+
+    def sums(slots, n):
+        return sum_copy(slots, slots, n, (group_at, member_at))
+
+    in_plane = sums(member_sums.at[pl.ds(1, members - 1), row], 0)
+    from_later = sums(direct.at[pl.ds(1, groups - 1)], 2)
+    from_earlier = sums(group_sums.at[pl.ds(1, groups - 1), row], 4)
 
     def first_round(n):
         dx, dy = SIDES[n]
@@ -298,28 +331,37 @@
                 all_of(rows, n, 0).wait_send()
 
     with phase("start1"):
-        for c in sum_copies(member_sums, 0, members, next_member):
-            c.start()
+        share_in_plane()
+        share_with_earlier()
         start(first_round)
-        fill(first_round)
-        fill(second_coarse)
-        fill(early_fine)
-        fill(late_fine)
+        lax.fori_loop(0, group_at, report, 0)
+    with phase("fill"):
+        fill_sums()
+        for round_of in (first_round, second_coarse, early_fine, late_fine):
+            fill(round_of)
 
     with phase("w_msum"):
-        sum_total(member_sums, 0, members).wait_recv()
+        in_plane.wait_recv()
     part = member_sums[0, row, :]
     for o in range(1, members):
         part = part + member_sums[o, row, :]
     group_sums[0, row, :] = part
-    for c in sum_copies(group_sums, 2, groups, next_group):
-        c.start()
+    with phase("w_ready"):
+        @pl.when(group_at < groups - 1)
+        def _():
+            pl.semaphore_wait(ready, groups - 1 - group_at)
+    share_with_later()
     with phase("w_gsum"):
-        sum_total(group_sums, 2, groups).wait_recv()
+        from_earlier.wait_recv()
+    with phase("w_direct"):
+        from_later.wait_recv()
     with phase("mean"):
         total = group_sums[0, row, :]
+        later = jnp.zeros((members, cz), f32)
         for o in range(1, groups):
             total = total + group_sums[o, row, :]
+            later = later + direct[o]
+        total = total + jnp.sum(later, axis=0, keepdims=True)
         mean = jnp.sum(total) / (cx * cy * cz * groups * members)
     with phase("w_halo1"):
         arrive(first_round)
@@ -456,8 +498,9 @@
 
     with phase("w_sent"):
         sent(first_round, second_coarse, early_fine, late_fine)
-        sum_total(member_sums, 0, members).wait_send()
-        sum_total(group_sums, 2, groups).wait_send()
+        in_plane.wait_send()
+        from_later.wait_send()
+        from_earlier.wait_send()
 
 
 def put(red, post, defect, contrast, smoothed_out, residual_out, smoothed, residual, sem):
@@ -524,12 +567,14 @@
             pltpu.VMEM((3, hy + 16, cz), f32),
             pltpu.VMEM((members, 8, cz), f32),
             pltpu.VMEM((groups, 8, cz), f32),
+            pltpu.VMEM((groups, members, cz), f32),
             pltpu.VMEM((2, px, cy, cz), f32),
             pltpu.VMEM((64 * cy, cz), f32),
             dma((3,)),
             dma((len(SIDES),)),
             dma((3,)),
-            dma((4,)),
+            dma((6,)),
+            pltpu.SemaphoreType.REGULAR,
         ],
         compiler_params=pltpu.CompilerParams(collective_id=0, has_side_effects=True),
     )(refined, source, potential)

time: 21.2 us -> 19.7 us (0.929)
  the two profiles are of different devices: /device:TPU:0 before, /device:TPU:1 now
where the time goes in v3:
time: 19.7 us; the launch traced here: 19.5 us
  Pallas kernels  18.9 us (96%)
  between operations  0.64 us (3%)
    pallas_call x1, Pallas kernels, per_device(): pl.pallas_call(functools.partial(kernel, dims, (cx, cy, cz)), out_shape=[...  17.8 us
    pallas_call x1, Pallas kernels, per_device(): pl.pallas_call(put, out_shape=[jax.ShapeDtypeStruct(source.shape, f32)] *...  1.11 us

profile of v3, /device:TPU:1, one launch (start us, length us, event | category | flops | bytes accessed | tf_op | source)
XLA Modules:
  0.0 19.5 jit_solution(3215394825471521317)
XLA Ops:
  0.6 17.8 %shard_map.50 = (f32[22,56,128]{2,1,0:T(8,128)S(1)}, f32[22,56,128]{2,1,0:T(8,128)S(1)}, f32[16,40,128]{2,1,0:T(8,128)S(1)}, f32[16,32,128]{2,1,0:T(8,128)S(1)}) custom-call(s32[1,1,4]{2,1,0:T(1,128)} %refined_hbm.1, f32[32,32,128]{2,1,0:T(8,128)} %source_ref.1, f32[32,32,128]{2,1,0:T(8,128)} %potential_ref.1), custom_call_target="tpu_custom_call" | custom-call | tf_op jit(solution)/shard_map/pallas_call | solution.py:542
  18.4 1.1 %shard_map.51 = (f32[32,32,128]{2,1,0:T(8,128)}, f32[32,32,128]{2,1,0:T(8,128)}) custom-call(f32[22,56,128]{2,1,0:T(8,128)S(1)} %get-tuple-element.6.red, f32[22,56,128]{2,1,0:T(8,128)S(1)} %get-tuple-element.7.post, f32[16,40,128]{2,1,0:T(8,128)S(1)} %get-tuple-element.8.defect, f32[16,32,128]{2,1,0:T(8,128)S(1)} %get-tuple-element.9.contrast), custom_call_target="tpu_custom_call" | custom-call | tf_op jit(solution)/shard_map/pallas_call | solution.py:581

commit v4 on v3

--- a/solution.py
+++ b/solution.py
@@ -177,6 +177,8 @@
         signal(ready, (g, member_at))
         return carry
 
+    lax.fori_loop(0, group_at, report, 0)
+
     row = pl.ds(0, 1)
 
     def sum_copy(src, dst, n, at):
@@ -253,26 +255,20 @@
             pairs.append((mixed.at[sx, sy], mixed.at[tx, ty]))
         return 1, pairs
 
-    def second_fine(n, early):
+    def second_fine(n):
         dx, dy = SIDES[n]
         if dx and dy:
-            pieces = () if early else ((0, 1, 0, 4), (1, 2, 0, 2))
+            pieces = ((0, 1, 0, 4), (1, 2, 0, 2))
         elif dx:
-            pieces = () if early else ((0, HALO, 0, cy),)
+            pieces = ((0, HALO, 0, cy),)
         else:
-            pieces = ((0, px // 2, 1, REACH + 1),) if early else ((px // 2, px, 1, REACH + 1),)
+            pieces = ((0, px, 1, REACH + 1),)
         pairs = []
         for begin, end, skip, deep in pieces:
-            if dx:
-                sx, tx = span(dx, begin, end, HALO, px)
-            else:
-                sx = tx = pl.ds(HALO + begin, end - begin)
+            sx, tx = span(dx, begin, end, HALO, px)
             sy, ty = span(dy, skip, deep, ROW0, cy)
             pairs.append((mid.at[sx, sy], landed.at[tx, ty]))
         return 2, pairs
-
-    early_fine = functools.partial(second_fine, early=True)
-    late_fine = functools.partial(second_fine, early=False)
 
     def rows_of(pairs):
         total = 0
@@ -280,26 +276,29 @@
             total += functools.reduce(lambda p, q: p * q, dst.shape[:-1])
         return total
 
+    odd = lax.rem(member_at, 2) == 1
+
     def start(round_of):
-        for n, (dx, dy) in enumerate(SIDES):
-            kind, pairs = round_of(n)
-            if not pairs:
-                continue
-
-            @pl.when(there(dx, dy))
-            def _():
-                for src, dst in pairs:
-                    pltpu.make_async_remote_copy(
-                        src_ref=src, dst_ref=dst, send_sem=send_sem.at[n], recv_sem=recv_sem.at[kind],
-                        device_id=device(dx, dy), device_id_type=MESH,
-                    ).start()
+        for far in (True, None, False):
+            for n, (dx, dy) in enumerate(SIDES):
+                if (dy == 0) != (far is None):
+                    continue
+                kind, pairs = round_of(n)
+                now = there(dx, dy)
+                if far is not None:
+                    now = now & (odd if (dy > 0) == far else jnp.logical_not(odd))
+
+                @pl.when(now)
+                def _():
+                    for src, dst in pairs:
+                        pltpu.make_async_remote_copy(
+                            src_ref=src, dst_ref=dst, send_sem=send_sem.at[n], recv_sem=recv_sem.at[kind],
+                            device_id=device(dx, dy), device_id_type=MESH,
+                        ).start()
 
     def fill(round_of):
         for n, (dx, dy) in enumerate(SIDES):
             kind, pairs = round_of(n)
-            if not pairs:
-                continue
-
             @pl.when(jnp.logical_not(there(-dx, -dy)))
             def _():
                 for _, dst in pairs:
@@ -334,10 +333,9 @@
         share_in_plane()
         share_with_earlier()
         start(first_round)
-        lax.fori_loop(0, group_at, report, 0)
     with phase("fill"):
         fill_sums()
-        for round_of in (first_round, second_coarse, early_fine, late_fine):
+        for round_of in (first_round, second_coarse, second_fine):
             fill(round_of)
 
     with phase("w_msum"):
@@ -408,9 +406,6 @@
             centre = red[HALO + a, own_rows, :]
             yield a, centre, own_rhs[a] - mean + nbr - 6.0 * centre
 
-    with phase("start_early"):
-        start(early_fine)
-
     with phase("restrict"):
         for first in range(0, px, 4):
             for a, centre, res in red_defects(mid, range(first, first + 4)):
@@ -427,7 +422,7 @@
 
     with phase("start2"):
         start(second_coarse)
-        start(late_fine)
+        start(second_fine)
         for a in range(px):
             own_rhs[a] = own_rhs[a] - mean
     with phase("w_coarse"):
@@ -461,7 +456,7 @@
                         out[a, coarse_rows, :] = (right[a, coarse_rows, :] + nbr) * weight
 
     with phase("w_fine2"):
-        arrive(early_fine, late_fine)
+        arrive(second_fine)
 
     with phase("prolong"):
         half_rows = hy + 8
@@ -497,7 +492,7 @@
         half_sweep(3, black_rhs, post, red, post, defect)
 
     with phase("w_sent"):
-        sent(first_round, second_coarse, early_fine, late_fine)
+        sent(first_round, second_coarse, second_fine)
         in_plane.wait_send()
         from_later.wait_send()
         from_earlier.wait_send()

time: 19.7 us -> 18.7 us (0.949)
  the two profiles are of different devices: /device:TPU:1 before, /device:TPU:0 now
where the time goes in v4:
time: 18.7 us; the launch traced here: 18.5 us
  Pallas kernels  17.8 us (95%)
  between operations  0.64 us (3%)
    pallas_call x1, Pallas kernels, per_device(): pl.pallas_call(functools.partial(kernel, dims, (cx, cy, cz)), out_shape=[...  16.7 us
    pallas_call x1, Pallas kernels, per_device(): pl.pallas_call(put, out_shape=[jax.ShapeDtypeStruct(source.shape, f32)] *...  1.11 us

profile of v4, /device:TPU:0, one launch (start us, length us, event | category | flops | bytes accessed | tf_op | source)
XLA Modules:
  0.0 18.5 jit_solution(4576769326005151847)
XLA Ops:
  0.6 16.7 %shard_map.50 = (f32[22,56,128]{2,1,0:T(8,128)S(1)}, f32[22,56,128]{2,1,0:T(8,128)S(1)}, f32[16,40,128]{2,1,0:T(8,128)S(1)}, f32[16,32,128]{2,1,0:T(8,128)S(1)}) custom-call(s32[1,1,4]{2,1,0:T(1,128)} %refined_hbm.1, f32[32,32,128]{2,1,0:T(8,128)} %source_ref.1, f32[32,32,128]{2,1,0:T(8,128)} %potential_ref.1), custom_call_target="tpu_custom_call" | custom-call | tf_op jit(solution)/shard_map/pallas_call | solution.py:537
  17.4 1.1 %shard_map.51 = (f32[32,32,128]{2,1,0:T(8,128)}, f32[32,32,128]{2,1,0:T(8,128)}) custom-call(f32[22,56,128]{2,1,0:T(8,128)S(1)} %get-tuple-element.6.red, f32[22,56,128]{2,1,0:T(8,128)S(1)} %get-tuple-element.7.post, f32[16,40,128]{2,1,0:T(8,128)S(1)} %get-tuple-element.8.defect, f32[16,32,128]{2,1,0:T(8,128)S(1)} %get-tuple-element.9.contrast), custom_call_target="tpu_custom_call" | custom-call | tf_op jit(solution)/shard_map/pallas_call | solution.py:576

commit v5 on v4

--- a/solution.py
+++ b/solution.py
@@ -20,6 +20,7 @@
 SIDES = ((0, -1), (0, 1), (-1, 0), (1, 0), (-1, -1), (-1, 1), (1, -1), (1, 1))
 MESH = pl.DeviceIdType.MESH
 SIXTH = 1.0 / 6.0
+DETOUR = 2
 PIECES = 4
 
 
@@ -67,8 +68,8 @@
     refined_hbm, source_ref, potential_ref,
     red, post, defect, own_rhs,
     refined_ref, raw, field, mid, landed, pair_rows, mixed, rhs0, rhs1, corr0, corr1, wide,
-    flags, active, inside, member_sums, group_sums, direct, zeros, dummy,
-    local_sem, send_sem, recv_sem, sum_sem, ready,
+    flags, active, inside, member_sums, group_sums, direct, passing, unit_red, unit_black, zeros, dummy,
+    local_sem, send_sem, recv_sem, sum_sem, pass_sem, ready,
 ):
     groups, members = dims
     cx, cy, cz = sizes
@@ -225,9 +226,13 @@
     from_later = sums(direct.at[pl.ds(1, groups - 1)], 2)
     from_earlier = sums(group_sums.at[pl.ds(1, groups - 1), row], 4)
 
+    def marks_round(n):
+        dx, dy = SIDES[n]
+        return 4, [(flags.at[1, 1, row], flags.at[1 - dx, 1 - dy, row])]
+
     def first_round(n):
         dx, dy = SIDES[n]
-        pairs = [(flags.at[1, 1, row], flags.at[1 - dx, 1 - dy, row])]
+        pairs = []
         if dx and dy:
             pieces = ((0, 1, 0, 1, 4), (1, 1, 0, 1, 3), (2, 1, 0, 1, 2), (0, 1, 1, 2, 2), (1, 1, 1, 2, 1))
         elif dx:
@@ -238,7 +243,7 @@
             sx, tx = span(dx, begin, end, HALO, px)
             sy, ty = span(dy, 0, deep, ROW0, cy)
             pairs.append((field.at[pl.ds(kind, kinds), sx, sy], field.at[pl.ds(kind, kinds), tx, ty]))
-        return 0, pairs
+        return (3 if dy else 0), pairs
 
     def second_coarse(n):
         dx, dy = SIDES[n]
@@ -290,11 +295,60 @@
 
                 @pl.when(now)
                 def _():
-                    for src, dst in pairs:
+                    split = via and far and not dx and round_of is first_round
+                    if split:
+                        send_face(n)
+                    for src, dst in () if split else pairs:
                         pltpu.make_async_remote_copy(
                             src_ref=src, dst_ref=dst, send_sem=send_sem.at[n], recv_sem=recv_sem.at[kind],
                             device_id=device(dx, dy), device_id_type=MESH,
                         ).start()
+
+    around = px * DETOUR // 8
+    via = members % 2 == 0
+    detour = []
+    at_row = 0
+    for kind, deep in ((0, REACH + 1), (1, REACH), (2, REACH - 1)):
+        detour.append((kind, deep, pl.ds(at_row, deep)))
+        at_row += deep
+    detour_rows = at_row * around
+    direct_planes, around_planes = pl.ds(HALO, px - around), pl.ds(HALO + px - around, around)
+
+    def send_face(n):
+        dx, dy = SIDES[n]
+        for by_detour in (True, False):
+            for kind, deep, rows in detour:
+                sy, ty = span(dy, 0, deep, ROW0, cy)
+                planes = around_planes if by_detour else direct_planes
+                pltpu.make_async_remote_copy(
+                    src_ref=field.at[kind, planes, sy],
+                    dst_ref=passing.at[pl.ds(0, around), rows] if by_detour else field.at[kind, planes, ty],
+                    send_sem=send_sem.at[n], recv_sem=pass_sem.at[0] if by_detour else recv_sem.at[3],
+                    device_id=device(0, 2 * dy if by_detour else dy), device_id_type=MESH,
+                ).start()
+
+    def passes(side):
+        return (odd & (member_at >= 2)) if side < 0 else (jnp.logical_not(odd) & (member_at + 2 < members))
+
+    def passed():
+        part = dummy.at[pl.ds(0, detour_rows)]
+        return pltpu.make_async_remote_copy(
+            src_ref=part, dst_ref=part, send_sem=pass_sem.at[1], recv_sem=pass_sem.at[0],
+            device_id=(group_at, member_at), device_id_type=MESH,
+        )
+
+    def pass_on(now):
+        for side in (-1, 1):
+            @pl.when(passes(side) & now)
+            def _():
+                passed().wait_recv()
+                for kind, deep, rows in detour:
+                    ty = span(-side, 0, deep, ROW0, cy)[1]
+                    pltpu.make_async_remote_copy(
+                        src_ref=passing.at[pl.ds(0, around), rows], dst_ref=field.at[kind, around_planes, ty],
+                        send_sem=pass_sem.at[1], recv_sem=recv_sem.at[3],
+                        device_id=device(0, side), device_id_type=MESH,
+                    ).start()
 
     def fill(round_of):
         for n, (dx, dy) in enumerate(SIDES):
@@ -313,13 +367,9 @@
             device_id=(group_at, member_at), device_id_type=MESH,
         )
 
-    def arrive(*rounds):
-        rows, kind = 0, None
-        for round_of in rounds:
-            for n in range(len(SIDES)):
-                kind, pairs = round_of(n)
-                rows += rows_of(pairs)
-        all_of(rows, 0, kind).wait_recv()
+    def arrive(round_of, kind):
+        arriving = (round_of(n) for n in range(len(SIDES)))
+        all_of(sum(rows_of(pairs) for which, pairs in arriving if which == kind), 0, kind).wait_recv()
 
     def sent(*rounds):
         for n, (dx, dy) in enumerate(SIDES):
@@ -332,10 +382,11 @@
     with phase("start1"):
         share_in_plane()
         share_with_earlier()
+        start(marks_round)
         start(first_round)
     with phase("fill"):
         fill_sums()
-        for round_of in (first_round, second_coarse, second_fine):
+        for round_of in (marks_round, first_round, second_coarse, second_fine):
             fill(round_of)
 
     with phase("w_msum"):
@@ -344,11 +395,86 @@
     for o in range(1, members):
         part = part + member_sums[o, row, :]
     group_sums[0, row, :] = part
+    if via:
+        with phase("pass1"):
+            pass_on(group_at < 2)
     with phase("w_ready"):
         @pl.when(group_at < groups - 1)
         def _():
             pl.semaphore_wait(ready, groups - 1 - group_at)
     share_with_later()
+    if via:
+        with phase("pass2"):
+            pass_on(group_at >= 2)
+    def plane_groups(t):
+        wide_by = (REACH - t + 1) // 2
+        for region, low, high in ((0, HALO - wide_by, HALO), (1, HALO, HALO + px), (2, HALO + px, HALO + px + wide_by)):
+            for first in range(low, high, 4):
+                yield region, range(first, min(first + 4, high))
+
+    fine_mask = checker(window, cz)
+    stages = ((mix, mix, black, red), (black_rhs, black, red, mid), (mix, red, mid, red), (black_rhs, mid, red, mid))
+
+    with phase("w_marks"):
+        arrive(marks_round, 4)
+    with phase("masks"):
+        edge = lax.broadcasted_iota(jnp.int32, (8, cz), 0) < REACH
+        for x in range(3):
+            low, own, high = flags[x, 0], flags[x, 1], flags[x, 2]
+            low, own, high = (jnp.broadcast_to(v[0:1], (8, cz)) for v in (low, own, high))
+            active[x, pl.ds(0, 8), :] = jnp.where(edge, low, own)
+            for t in range(1, window // 8 - 1):
+                active[x, pl.ds(8 * t, 8), :] = own
+            active[x, pl.ds(window - 8, 8), :] = jnp.where(edge, own, high)
+
+    with phase("unit"):
+        rows = pl.ds(ROW0 - REACH, window)
+        for p in range(HALO - 2, HALO + px + 2):
+            region = 0 if p < HALO else 1 if p < HALO + px else 2
+            unit_red[p, rows, :] = active[region] * SIXTH
+        for t, other, out in ((1, unit_red, unit_black), (2, unit_black, unit_red)):
+            for region, planes in plane_groups(t):
+                weight = active[region] * SIXTH
+                sums = neighbours(other, planes, ROW0 - REACH, window, t % 2, fine_mask, 1)
+                for p, nbr in zip(planes, sums):
+                    out[p, rows, :] = (1.0 + nbr) * weight
+
+    with phase("w_along"):
+        arrive(first_round, 0)
+    with phase("inner"):
+        inner = cy - 2
+        inner_rows = pl.ds(ROW0 + 1, inner)
+        at = lax.broadcasted_iota(jnp.int32, (inner, cz), 0)
+        inner_mask = jnp.logical_not(checker(inner, cz))
+        smoothed = [jnp.broadcast_to(flags[x, 1, row, :], (inner, cz)) > 0.5 for x in range(3)]
+        for t, (right, old, other, out) in enumerate(stages[:-1]):
+            reached = (at >= t) & (at < inner - t)
+            for region, planes in plane_groups(t):
+                keep = smoothed[region] & reached
+                sums = neighbours(other, planes, ROW0 + 1, inner, t % 2, inner_mask, 1)
+                for p, nbr in zip(planes, sums):
+                    total = right[p, inner_rows, :] + nbr
+                    out[p, inner_rows, :] = jnp.where(keep, total * SIXTH, old[p, inner_rows, :])
+
+    with phase("w_halo1"):
+        arrive(first_round, 3)
+
+    with phase("edges"):
+        edge_mask = checker(8, cz)
+        sub = lax.broadcasted_iota(jnp.int32, (8, cz), 0)
+        for t, (right, old, other, out) in enumerate(stages[:-1]):
+            for region, planes in plane_groups(t):
+                for low in (True, False):
+                    first = ROW0 - REACH if low else ROW0 + cy - REACH
+                    rows = pl.ds(first, 8)
+                    keep = active[region, pl.ds(first - ROW0 + REACH, 8), :] > 0.5
+                    fresh = (sub <= REACH + t) if low else (sub >= REACH - 1 - t)
+                    sums = neighbours(other, planes, first, 8, t % 2, edge_mask, 1)
+                    for p, nbr in zip(planes, sums):
+                        total = right[p, rows, :] + nbr
+                        value = jnp.where(keep, total * SIXTH, old[p, rows, :])
+                        out[p, rows, :] = jnp.where(fresh, value, out[p, rows, :])
+
     with phase("w_gsum"):
         from_earlier.wait_recv()
     with phase("w_direct"):
@@ -361,42 +487,24 @@
             later = later + direct[o]
         total = total + jnp.sum(later, axis=0, keepdims=True)
         mean = jnp.sum(total) / (cx * cy * cz * groups * members)
-    with phase("w_halo1"):
-        arrive(first_round)
-
-    with phase("masks"):
-        edge = lax.broadcasted_iota(jnp.int32, (8, cz), 0) < REACH
-        for x in range(3):
-            low, own, high = flags[x, 0], flags[x, 1], flags[x, 2]
-            low, own, high = (jnp.broadcast_to(v[0:1], (8, cz)) for v in (low, own, high))
-            active[x, pl.ds(0, 8), :] = jnp.where(edge, low, own)
-            for t in range(1, window // 8 - 1):
-                active[x, pl.ds(8 * t, 8), :] = own
-            active[x, pl.ds(window - 8, 8), :] = jnp.where(edge, own, high)
-
-    fine_mask = checker(window, cz)
-
-    def half_sweep(t, right, old, other, out, also=None):
-        colour = t % 2
-        wide_by = (REACH - t + 1) // 2
+
+    def black_sweep(right, other, out):
         rows = pl.ds(ROW0 - REACH, window)
-        for region, low, high in ((0, HALO - wide_by, HALO), (1, HALO, HALO + px), (2, HALO + px, HALO + px + wide_by)):
+        for region, planes in plane_groups(REACH - 1):
             keep = active[region] > 0.5
-            for first in range(low, high, 4):
-                planes = range(first, min(first + 4, high))
-                sums = neighbours(other, planes, ROW0 - REACH, window, colour, fine_mask, 1)
-                for p, nbr in zip(planes, sums):
-                    total = right[p, rows, :] - mean + nbr
-                    before = old[p, rows, :]
-                    out[p, rows, :] = jnp.where(keep, total * SIXTH, before)
-                    if also is not None and region == 1:
-                        also[p - HALO] = jnp.where(keep, 0.0, total - 6.0 * before)
-
-    with phase("pre"):
-        half_sweep(0, mix, mix, black, red)
-        half_sweep(1, black_rhs, black, red, mid)
-        half_sweep(2, mix, mix, mid, red)
-        half_sweep(3, black_rhs, black, red, mid, defect)
+            sums = neighbours(other, planes, ROW0 - REACH, window, 1, fine_mask, 1)
+            for p, nbr in zip(planes, sums):
+                total = right[p, rows, :] - mean + nbr
+                before = out[p, rows, :]
+                out[p, rows, :] = jnp.where(keep, total * SIXTH, before)
+                if region == 1:
+                    defect[p - HALO] = jnp.where(keep, 0.0, total - 6.0 * before)
+
+    with phase("last_pre"):
+        rows = pl.ds(ROW0 - REACH, window)
+        for p in range(HALO - 1, HALO + px + 1):
+            red[p, rows, :] = red[p, rows, :] - mean * unit_red[p, rows, :]
+        black_sweep(black_rhs, red, mid)
 
     own_mask = checker(cy, cz)
 
@@ -426,7 +534,7 @@
         for a in range(px):
             own_rhs[a] = own_rhs[a] - mean
     with phase("w_coarse"):
-        arrive(second_coarse)
+        arrive(second_coarse, 1)
 
     with phase("coarse"):
         coarse_rows = pl.ds(CROW0 - 8, cwindow)
@@ -456,7 +564,7 @@
                         out[a, coarse_rows, :] = (right[a, coarse_rows, :] + nbr) * weight
 
     with phase("w_fine2"):
-        arrive(second_fine)
+        arrive(second_fine, 2)
 
     with phase("prolong"):
         half_rows = hy + 8
@@ -486,13 +594,24 @@
                 red[p, high_rows, :] = red[p, high_rows, :] + high
 
     with phase("post"):
-        half_sweep(0, mix, red, post, red)
-        half_sweep(1, black_rhs, post, red, post)
-        half_sweep(2, mix, red, post, red)
-        half_sweep(3, black_rhs, post, red, post, defect)
+        rows = pl.ds(ROW0 - REACH, window)
+        for t in range(REACH - 1):
+            right, other, out = (black_rhs, red, post) if t % 2 else (mix, post, red)
+            for region, planes in plane_groups(t):
+                keep = active[region] > 0.5
+                sums = neighbours(other, planes, ROW0 - REACH, window, t % 2, fine_mask, 1)
+                for p, nbr in zip(planes, sums):
+                    total = right[p, rows, :] - mean + nbr
+                    out[p, rows, :] = jnp.where(keep, total * SIXTH, out[p, rows, :])
+        black_sweep(black_rhs, red, post)
 
     with phase("w_sent"):
-        sent(first_round, second_coarse, second_fine)
+        sent(marks_round, first_round, second_coarse, second_fine)
+        if via:
+            for side in (-1, 1):
+                @pl.when(passes(side))
+                def _():
+                    passed().wait_send()
         in_plane.wait_send()
         from_later.wait_send()
         from_earlier.wait_send()
@@ -502,24 +621,27 @@
     px, cy, cz = contrast.shape
     own_rows = pl.ds(ROW0, cy)
     mask = checker(cy, cz)
+    copies = []
+
+    def send(n, src, dst, first, size):
+        part = pl.ds(2 * first, 2 * size)
+        copies.append(pltpu.make_async_copy(src.at[part], dst.at[part], sem.at[n]))
+        copies[-1].start()
+
+    for a in range(px):
+        centre, value = red[HALO + a, own_rows, :], post[HALO + a, own_rows, :]
+        smoothed[2 * a] = jnp.where(mask, centre, value)
+        smoothed[2 * a + 1] = jnp.where(mask, value, centre)
+    send(0, smoothed, smoothed_out, 0, px)
     size = px // PIECES
-    copies = []
     for piece in range(PIECES):
         planes = range(piece * size, (piece + 1) * size)
-        part = pl.ds(2 * piece * size, 2 * size)
-        for a in planes:
-            centre, value = red[HALO + a, own_rows, :], post[HALO + a, own_rows, :]
-            smoothed[2 * a] = jnp.where(mask, centre, value)
-            smoothed[2 * a + 1] = jnp.where(mask, value, centre)
-        copies.append(pltpu.make_async_copy(smoothed.at[part], smoothed_out.at[part], sem.at[0, piece]))
-        copies[-1].start()
         sums = neighbours(post, [HALO + a for a in planes], ROW0, cy, 0, mask, 1)
         for a, nbr in zip(planes, sums):
             res, other = contrast[a] + nbr - 6.0 * red[HALO + a, own_rows, :], defect[a, pl.ds(REACH, cy), :]
             residual[2 * a] = jnp.where(mask, res, other)
             residual[2 * a + 1] = jnp.where(mask, other, res)
-        copies.append(pltpu.make_async_copy(residual.at[part], residual_out.at[part], sem.at[1, piece]))
-        copies[-1].start()
+        send(1 + piece, residual, residual_out, piece * size, size)
     for c in copies:
         c.wait()
 
@@ -563,12 +685,16 @@
             pltpu.VMEM((members, 8, cz), f32),
             pltpu.VMEM((groups, 8, cz), f32),
             pltpu.VMEM((groups, members, cz), f32),
+            pltpu.VMEM((px, 16, cz), f32),
+            pltpu.VMEM(fine, f32),
+            pltpu.VMEM(fine, f32),
             pltpu.VMEM((2, px, cy, cz), f32),
             pltpu.VMEM((64 * cy, cz), f32),
             dma((3,)),
             dma((len(SIDES),)),
-            dma((3,)),
+            dma((5,)),
             dma((6,)),
+            dma((2,)),
             pltpu.SemaphoreType.REGULAR,
         ],
         compiler_params=pltpu.CompilerParams(collective_id=0, has_side_effects=True),
@@ -578,7 +704,7 @@
         out_shape=[jax.ShapeDtypeStruct(source.shape, f32)] * 2,
         in_specs=[vmem_spec] * 4,
         out_specs=[any_spec] * 2,
-        scratch_shapes=[pltpu.VMEM(source.shape, f32), pltpu.VMEM(source.shape, f32), dma((2, PIECES))],
+        scratch_shapes=[pltpu.VMEM(source.shape, f32), pltpu.VMEM(source.shape, f32), dma((1 + PIECES,))],
     )(*(pltpu.with_memory_space_constraint(v, pltpu.VMEM) for v in results)))
 
 

time: 18.7 us -> 18.3 us (0.979)
  Pallas kernels: 17.8 us -> 17.4 us
    pallas_call x1, Pallas kernels: 16.7 us -> 16.3 us  [per_device(): pl.pallas_call(functools.partial(kernel, dims, (cx, cy, cz)), out_shape=[...]
where the time goes in v5:
time: 18.3 us; the launch traced here: 18 us
  Pallas kernels  17.4 us (95%)
  between operations  0.64 us (3%)
    pallas_call x1, Pallas kernels, per_device(): pl.pallas_call(functools.partial(kernel, dims, (cx, cy, cz)), out_shape=[...  16.3 us
    pallas_call x1, Pallas kernels, per_device(): pl.pallas_call(put, out_shape=[jax.ShapeDtypeStruct(source.shape, f32)] *...  1.08 us

profile of v5, /device:TPU:0, one launch (start us, length us, event | category | flops | bytes accessed | tf_op | source)
XLA Modules:
  0.0 18.0 jit_solution(3609605824278976875)
XLA Ops:
  0.6 16.3 %shard_map.50 = (f32[22,56,128]{2,1,0:T(8,128)S(1)}, f32[22,56,128]{2,1,0:T(8,128)S(1)}, f32[16,40,128]{2,1,0:T(8,128)S(1)}, f32[16,32,128]{2,1,0:T(8,128)S(1)}) custom-call(s32[1,1,4]{2,1,0:T(1,128)} %refined_hbm.1, f32[32,32,128]{2,1,0:T(8,128)} %source_ref.1, f32[32,32,128]{2,1,0:T(8,128)} %potential_ref.1), custom_call_target="tpu_custom_call" | custom-call | tf_op jit(solution)/shard_map/pallas_call | solution.py:659
  16.9 1.1 %shard_map.51 = (f32[32,32,128]{2,1,0:T(8,128)}, f32[32,32,128]{2,1,0:T(8,128)}) custom-call(f32[22,56,128]{2,1,0:T(8,128)S(1)} %get-tuple-element.6.red, f32[22,56,128]{2,1,0:T(8,128)S(1)} %get-tuple-element.7.post, f32[16,40,128]{2,1,0:T(8,128)S(1)} %get-tuple-element.8.defect, f32[16,32,128]{2,1,0:T(8,128)S(1)} %get-tuple-element.9.contrast), custom_call_target="tpu_custom_call" | custom-call | tf_op jit(solution)/shard_map/pallas_call | solution.py:702

commit v6 on v5

--- a/solution.py
+++ b/solution.py
@@ -283,8 +283,8 @@
 
     odd = lax.rem(member_at, 2) == 1
 
-    def start(round_of):
-        for far in (True, None, False):
+    def start(round_of, order=(True, None, False)):
+        for far in order:
             for n, (dx, dy) in enumerate(SIDES):
                 if (dy == 0) != (far is None):
                     continue
@@ -456,6 +456,19 @@
                     total = right[p, inner_rows, :] + nbr
                     out[p, inner_rows, :] = jnp.where(keep, total * SIXTH, old[p, inner_rows, :])
 
+    with phase("w_gsum"):
+        from_earlier.wait_recv()
+    with phase("w_direct"):
+        from_later.wait_recv()
+    with phase("mean"):
+        total = group_sums[0, row, :]
+        later = jnp.zeros((members, cz), f32)
+        for o in range(1, groups):
+            total = total + group_sums[o, row, :]
+            later = later + direct[o]
+        total = total + jnp.sum(later, axis=0, keepdims=True)
+        mean = jnp.sum(total) / (cx * cy * cz * groups * members)
+
     with phase("w_halo1"):
         arrive(first_round, 3)
 
@@ -475,19 +488,6 @@
                         value = jnp.where(keep, total * SIXTH, old[p, rows, :])
                         out[p, rows, :] = jnp.where(fresh, value, out[p, rows, :])
 
-    with phase("w_gsum"):
-        from_earlier.wait_recv()
-    with phase("w_direct"):
-        from_later.wait_recv()
-    with phase("mean"):
-        total = group_sums[0, row, :]
-        later = jnp.zeros((members, cz), f32)
-        for o in range(1, groups):
-            total = total + group_sums[o, row, :]
-            later = later + direct[o]
-        total = total + jnp.sum(later, axis=0, keepdims=True)
-        mean = jnp.sum(total) / (cx * cy * cz * groups * members)
-
     def black_sweep(right, other, out):
         rows = pl.ds(ROW0 - REACH, window)
         for region, planes in plane_groups(REACH - 1):
@@ -530,7 +530,7 @@
 
     with phase("start2"):
         start(second_coarse)
-        start(second_fine)
+        start(second_fine, (False, None, True))
         for a in range(px):
             own_rhs[a] = own_rhs[a] - mean
     with phase("w_coarse"):

time: 18.3 us -> 18.1 us (0.989)
  Pallas kernels: 17.4 us -> 17.2 us
    pallas_call x1, Pallas kernels: 16.3 us -> 16.1 us  [per_device(): pl.pallas_call(functools.partial(kernel, dims, (cx, cy, cz)), out_shape=[...]
where the time goes in v6:
time: 18.1 us; the launch traced here: 17.8 us
  Pallas kernels  17.2 us (95%)
  between operations  0.64 us (4%)
    pallas_call x1, Pallas kernels, per_device(): pl.pallas_call(functools.partial(kernel, dims, (cx, cy, cz)), out_shape=[...  16.1 us
    pallas_call x1, Pallas kernels, per_device(): pl.pallas_call(put, out_shape=[jax.ShapeDtypeStruct(source.shape, f32)] *...  1.08 us

profile of v6, /device:TPU:0, one launch (start us, length us, event | category | flops | bytes accessed | tf_op | source)
XLA Modules:
  0.0 17.8 jit_solution(4400362362469103670)
XLA Ops:
  0.6 16.1 %shard_map.50 = (f32[22,56,128]{2,1,0:T(8,128)S(1)}, f32[22,56,128]{2,1,0:T(8,128)S(1)}, f32[16,40,128]{2,1,0:T(8,128)S(1)}, f32[16,32,128]{2,1,0:T(8,128)S(1)}) custom-call(s32[1,1,4]{2,1,0:T(1,128)} %refined_hbm.1, f32[32,32,128]{2,1,0:T(8,128)} %source_ref.1, f32[32,32,128]{2,1,0:T(8,128)} %potential_ref.1), custom_call_target="tpu_custom_call" | custom-call | tf_op jit(solution)/shard_map/pallas_call | solution.py:659
  16.7 1.1 %shard_map.51 = (f32[32,32,128]{2,1,0:T(8,128)}, f32[32,32,128]{2,1,0:T(8,128)}) custom-call(f32[22,56,128]{2,1,0:T(8,128)S(1)} %get-tuple-element.6.red, f32[22,56,128]{2,1,0:T(8,128)S(1)} %get-tuple-element.7.post, f32[16,40,128]{2,1,0:T(8,128)S(1)} %get-tuple-element.8.defect, f32[16,32,128]{2,1,0:T(8,128)S(1)} %get-tuple-element.9.contrast), custom_call_target="tpu_custom_call" | custom-call | tf_op jit(solution)/shard_map/pallas_call | solution.py:702

commit v7 on v6

--- a/solution.py
+++ b/solution.py
@@ -20,7 +20,7 @@
 SIDES = ((0, -1), (0, 1), (-1, 0), (1, 0), (-1, -1), (-1, 1), (1, -1), (1, 1))
 MESH = pl.DeviceIdType.MESH
 SIXTH = 1.0 / 6.0
-DETOUR = 2
+DETOUR = 3
 PIECES = 4
 
 
@@ -184,7 +184,7 @@
 
     def sum_copy(src, dst, n, at):
         return pltpu.make_async_remote_copy(
-            src_ref=src, dst_ref=dst, send_sem=sum_sem.at[n], recv_sem=sum_sem.at[n + 1], device_id=at, device_id_type=MESH,
+            src_ref=src, dst_ref=dst, send_sem=sum_sem.at[0], recv_sem=sum_sem.at[n], device_id=at, device_id_type=MESH,
         )
 
     own_sum, plane_sum = member_sums.at[0, row], group_sums.at[0, row]
@@ -192,7 +192,7 @@
 
     def share_in_plane():
         for o in range(1, members):
-            sum_copy(own_sum, member_sums.at[o, row], 0, (group_at, lax.rem(member_at + o, members))).start()
+            sum_copy(own_sum, member_sums.at[o, row], 1, (group_at, lax.rem(member_at + o, members))).start()
 
     def share_with_earlier():
         for o in range(groups - 1, 0, -1):
@@ -205,26 +205,27 @@
         for o in range(1, groups):
             @pl.when(group_at < o)
             def _():
-                pltpu.make_async_copy(zeros.at[0, 0, pl.ds(0, members)], dummy.at[pl.ds(o * members, members)], sum_sem.at[2]).start()
-                pltpu.make_async_copy(no_sum, group_sums.at[o, row], sum_sem.at[5]).start()
+                pltpu.make_async_copy(zeros.at[0, 0, pl.ds(0, members)], dummy.at[pl.ds(o * members, members)], sum_sem.at[0]).start()
+                pltpu.make_async_copy(no_sum, group_sums.at[o, row], sum_sem.at[3]).start()
 
             @pl.when(group_at + o >= groups)
             def _():
-                pltpu.make_async_copy(zeros.at[0, 0, pl.ds(0, members)], direct.at[o], sum_sem.at[3]).start()
-                pltpu.make_async_copy(no_sum, dummy.at[pl.ds(groups * members + o, 1)], sum_sem.at[4]).start()
+                pltpu.make_async_copy(zeros.at[0, 0, pl.ds(0, members)], direct.at[o], sum_sem.at[2]).start()
+                pltpu.make_async_copy(no_sum, dummy.at[pl.ds(groups * members + o, 1)], sum_sem.at[0]).start()
 
     def share_with_later():
         for o in range(1, groups):
             @pl.when(group_at + o < groups)
             def _():
-                sum_copy(plane_sum, group_sums.at[o, row], 4, (group_at + o, member_at)).start()
+                sum_copy(plane_sum, group_sums.at[o, row], 3, (group_at + o, member_at)).start()
 
     def sums(slots, n):
         return sum_copy(slots, slots, n, (group_at, member_at))
 
-    in_plane = sums(member_sums.at[pl.ds(1, members - 1), row], 0)
+    in_plane = sums(member_sums.at[pl.ds(1, members - 1), row], 1)
     from_later = sums(direct.at[pl.ds(1, groups - 1)], 2)
-    from_earlier = sums(group_sums.at[pl.ds(1, groups - 1), row], 4)
+    from_earlier = sums(group_sums.at[pl.ds(1, groups - 1), row], 3)
+    all_sums = sums(dummy.at[pl.ds(0, members - 1 + (groups - 1) * (members + 1))], 1)
 
     def marks_round(n):
         dx, dy = SIDES[n]
@@ -612,9 +613,7 @@
                 @pl.when(passes(side))
                 def _():
                     passed().wait_send()
-        in_plane.wait_send()
-        from_later.wait_send()
-        from_earlier.wait_send()
+        all_sums.wait_send()
 
 
 def put(red, post, defect, contrast, smoothed_out, residual_out, smoothed, residual, sem):
@@ -693,7 +692,7 @@
             dma((3,)),
             dma((len(SIDES),)),
             dma((5,)),
-            dma((6,)),
+            dma((4,)),
             dma((2,)),
             pltpu.SemaphoreType.REGULAR,
         ],

time: 18.1 us -> 18 us (level)
  no operation moved by 1% of the time
where the time goes in v7:
time: 18 us; the launch traced here: 17.7 us
  Pallas kernels  17.1 us (95%)
  between operations  0.64 us (4%)
    pallas_call x1, Pallas kernels, per_device(): pl.pallas_call(functools.partial(kernel, dims, (cx, cy, cz)), out_shape=[...  16 us
    pallas_call x1, Pallas kernels, per_device(): pl.pallas_call(put, out_shape=[jax.ShapeDtypeStruct(source.shape, f32)] *...  1.08 us

profile of v7, /device:TPU:0, one launch (start us, length us, event | category | flops | bytes accessed | tf_op | source)
XLA Modules:
  0.0 17.7 jit_solution(10916437683214389111)
XLA Ops:
  0.6 16.0 %shard_map.50 = (f32[22,56,128]{2,1,0:T(8,128)S(1)}, f32[22,56,128]{2,1,0:T(8,128)S(1)}, f32[16,40,128]{2,1,0:T(8,128)S(1)}, f32[16,32,128]{2,1,0:T(8,128)S(1)}) custom-call(s32[1,1,4]{2,1,0:T(1,128)} %refined_hbm.1, f32[32,32,128]{2,1,0:T(8,128)} %source_ref.1, f32[32,32,128]{2,1,0:T(8,128)} %potential_ref.1), custom_call_target="tpu_custom_call" | custom-call | tf_op jit(solution)/shard_map/pallas_call | solution.py:658
  16.7 1.1 %shard_map.51 = (f32[32,32,128]{2,1,0:T(8,128)}, f32[32,32,128]{2,1,0:T(8,128)}) custom-call(f32[22,56,128]{2,1,0:T(8,128)S(1)} %get-tuple-element.6.red, f32[22,56,128]{2,1,0:T(8,128)S(1)} %get-tuple-element.7.post, f32[16,40,128]{2,1,0:T(8,128)S(1)} %get-tuple-element.8.defect, f32[16,32,128]{2,1,0:T(8,128)S(1)} %get-tuple-element.9.contrast), custom_call_target="tpu_custom_call" | custom-call | tf_op jit(solution)/shard_map/pallas_call | solution.py:701
